TPU v7x, 256 devices: a 8x8x2 block of a 8x8x16 slice. The times are simulated.
256 devices in a mesh: grp: 2 (over z), spec: 128 (over x, y, core).
Axes of the slice: x: 8, y: 8, z: 2, core: 2. Of those that a mesh axis runs over, the one named last changes fastest.
The devices are a block of a 8x8x16 slice.
Arguments:
- spectrum: float32 [3072, 12288], P(('grp', 'spec')), parts along dimension 0, may hold values from 0.05 to 5
- sea_mask: int32 [12288], replicated, may hold values from 0 to 1, as said below
- wind_speed: float32 [24576], P('grp'), parts along dimension 0, may hold values from 0.3 to 3
- wind_angle: float32 [24576], P('grp'), parts along dimension 0, may hold values from -3.140625 to 3.140625
Outputs:
- new_spectrum: float32 [3072, 12288], P(('grp', 'spec')), parts along dimension 0
- wave_height: float32 [24576], P(('grp', 'spec')), parts along dimension 0
- mean_height: float32 [2], P('grp'), parts along dimension 0
There are 2 independent parts, one for each index of `grp`. A program takes and returns all parts, laid end to end along the dimension named above; an argument that names none is the same for every part. Nothing has to cross between parts.
Inputs may be any that keep to these rules, and one draw needn't show every extreme that they name: `sea_mask`: exactly 8192 cells are sea.
All inputs are finite; a program needn't handle non-finite values.
Results may differ from a plain program's by a relative error of at most 0.00002.
Values sent between devices are 32-bit elements; how exact they have to be, the bound alone decides.
A program may use at most 64 MiB of HBM per device.

v0:
```python
import math

import jax
import jax.numpy as jnp
from jax import lax
from jax.sharding import Mesh
from jax.sharding import PartitionSpec as P

NF = 48
ND = 32
NLON = 384
ADV_STEPS = 2
SEA_DEV = 64
SPEC = ("spec_0", "spec_1", "spec_2")
GRP_SPEC = ("grp", "spec_0", "spec_1", "spec_2")


def split_up(shard, dim, size):
    before, after = (shard.shape[:dim], shard.shape[dim + 1 :])
    return jnp.moveaxis(shard.reshape(*before, size, -1, *after), dim, 0)


def laid_out(pieces, dim):
    pieces = jnp.moveaxis(pieces, 0, dim)
    dims = pieces.shape
    return pieces.reshape(*dims[:dim], dims[dim] * dims[dim + 1], *dims[dim + 2 :])


def turned_blocks(pieces, axes, sequence):
    dims = [lax.axis_size(a) for a in axes]
    pieces = pieces.reshape(*dims, *pieces.shape[1:])
    for k in sequence:
        pieces = lax.all_to_all(pieces, axes[k], split_axis=k, concat_axis=k, tiled=True)
    return pieces.reshape(-1, *pieces.shape[len(axes) :])


def exchange_by_chip(shard, groups, sequence, split_dim, concat_dim):
    size = lax.axis_size(groups[0]) * lax.axis_size(groups[1])
    pieces = split_up(shard, split_dim, size)
    return laid_out(turned_blocks(pieces, groups, sequence), concat_dim)


def upwind_step(energy, courant_x, courant_y, sea_grid):
    west_cell = jnp.roll(energy, 1, axis=2)
    east_cell = jnp.roll(energy, -1, axis=2)
    edge_row = jnp.zeros_like(energy[:, :1])
    south_cell = jnp.concatenate([edge_row, energy[:, :-1]], axis=1)
    north_cell = jnp.concatenate([energy[:, 1:], edge_row], axis=1)
    updated = (
        energy
        - jnp.maximum(courant_x, 0.0) * (energy - west_cell)
        - jnp.minimum(courant_x, 0.0) * (east_cell - energy)
        - jnp.maximum(courant_y, 0.0) * (energy - south_cell)
        - jnp.minimum(courant_y, 0.0) * (north_cell - energy)
    )
    return updated * sea_grid


def courant_numbers(freq_index, dir_index, lat_count, dir_count):
    speed = 0.2 * jnp.exp(-math.log(1.1) * freq_index)
    heading = 2.0 * math.pi * (dir_index + 0.5) / dir_count
    rows = jnp.arange(lat_count, dtype=jnp.float32)
    latitude = (-75.0 + 150.0 * (rows + 0.5) / lat_count) * (math.pi / 180.0)
    courant_x = (speed * jnp.cos(heading))[:, None, None] / jnp.cos(latitude)[None, :, None]
    courant_y = (speed * jnp.sin(heading))[:, None, None]
    return (courant_x, courant_y)


def shift_freq(values, amount):
    if amount > 0:
        filler = jnp.zeros_like(values[:amount])
        return jnp.concatenate([filler, values[:-amount]], axis=0)
    filler = jnp.zeros_like(values[:-amount])
    return jnp.concatenate([values[-amount:], filler], axis=0)


def source_terms(energy, speed, angle):
    freq_count = energy.shape[0]
    dir_count = energy.shape[1]
    freq_ids = jnp.arange(freq_count, dtype=jnp.float32)
    frequency = jnp.exp(math.log(1.1) * (freq_ids - freq_count // 2))[:, None, None]
    heading = (2.0 * math.pi * (jnp.arange(dir_count, dtype=jnp.float32) + 0.5) / dir_count)[
        None, :, None
    ]
    energy_mean = jnp.mean(energy, axis=(0, 1))
    moment_one = jnp.mean(frequency * energy, axis=(0, 1))
    mean_freq = moment_one / (energy_mean + 1e-06)
    steepness = energy_mean * mean_freq * mean_freq
    breaking = steepness * steepness / (1.0 + steepness * steepness)
    wind_gain = (
        0.05
        * frequency
        * jnp.maximum(
            0.0, speed[None, None, :] * frequency * jnp.cos(heading - angle[None, None, :]) - 1.0
        )
    )
    damping = 0.03 * frequency * breaking[None, None, :]
    valid = ((freq_ids >= 3) & (freq_ids <= freq_count - 3)).astype(jnp.float32)[:, None, None]
    interaction = jnp.zeros_like(energy)
    for mirror in (1, -1):
        plus_bins = shift_freq(jnp.roll(energy, -mirror, axis=1), -2)
        minus_bins = shift_freq(jnp.roll(energy, 3 * mirror, axis=1), 3)
        transfer_rate = (
            0.001
            * valid
            * (energy * energy * (plus_bins + minus_bins) - 2.0 * energy * plus_bins * minus_bins)
        )
        interaction = interaction - 2.0 * transfer_rate
        interaction = interaction + jnp.roll(shift_freq(transfer_rate, 2), mirror, axis=1)
        interaction = interaction + jnp.roll(shift_freq(transfer_rate, -3), -3 * mirror, axis=1)
    updated = energy + (wind_gain - damping) * energy + interaction
    raw_height = 4.0 * jnp.sqrt(jnp.mean(updated, axis=(0, 1)) + 1e-06)
    return (updated, raw_height)


def local(spectrum, sea_mask, wind_speed, wind_angle):
    count = lax.axis_size(SPEC)
    position = lax.axis_index(SPEC)
    bins_dev = spectrum.shape[0]
    cells = spectrum.shape[1]
    points = cells // count
    lat_count = cells // NLON
    sea_float = sea_mask.astype(jnp.float32)
    bin_ids = position * bins_dev + jnp.arange(bins_dev, dtype=jnp.int32)
    freq_index = (bin_ids // ND).astype(jnp.float32)
    dir_index = (bin_ids % ND).astype(jnp.float32)
    courant_x, courant_y = courant_numbers(freq_index, dir_index, lat_count, ND)
    sea_grid = sea_float.reshape(1, lat_count, NLON)
    energy = (spectrum * sea_float[None, :]).reshape(bins_dev, lat_count, NLON)
    for substep in range(ADV_STEPS):
        energy = upwind_step(energy, courant_x, courant_y, sea_grid)
    advected = energy.reshape(bins_dev, cells)
    outgoing = advected.reshape(bins_dev, count, points)
    arrived = exchange_by_chip(outgoing, (("spec_0", "spec_1"), "spec_2"), (1, 0), 1, 0)
    start = position * points
    speed_own = lax.dynamic_slice_in_dim(wind_speed, start, points)
    angle_own = lax.dynamic_slice_in_dim(wind_angle, start, points)
    sea_own = lax.dynamic_slice_in_dim(sea_float, start, points)
    updated, raw_height = source_terms(arrived.reshape(NF, ND, points), speed_own, angle_own)
    wave_height = sea_own * raw_height
    own_total = jnp.zeros((count, 1), jnp.float32) + jnp.sum(wave_height)
    returned, totals = (
        lax.all_to_all(
            updated.reshape(NF * ND, 1, points), SPEC, split_axis=0, concat_axis=1, tiled=True
        ),
        lax.all_to_all(own_total, SPEC, split_axis=0, concat_axis=1, tiled=True),
    )
    new_spectrum = returned.reshape(bins_dev, cells)
    height_sum = jnp.sum(totals)
    mean_height = (height_sum / (SEA_DEV * count)).reshape(1)
    return (new_spectrum, wave_height, mean_height)


def solution(mesh):
    split = Mesh(
        mesh.devices.reshape(mesh.shape["grp"], 8, 8, 2), ("grp", "spec_0", "spec_1", "spec_2")
    )
    in_specs = (P(GRP_SPEC, None), P(), P("grp"), P("grp"))
    out_specs = (P(GRP_SPEC, None), P(GRP_SPEC), P("grp"))
    return jax.shard_map(local, mesh=split, in_specs=in_specs, out_specs=out_specs, check_vma=False)
```

profile of v0, /device:TPU:513, one launch (start us, length us, event | category | flops | bytes accessed | tf_op | source)
XLA Modules:
  0.0 123.7 jit_solution(12163557581757695200)
XLA Ops:
  0.8 0.8 convert_element_type.31
  1.6 1.2 broadcast_multiply_fusion
  3.1 0.2 fusion.33
  3.5 0.7 fusion.10
  4.5 0.2 fusion.36
  4.7 0.7 fusion.17
  5.4 0.2 reshape_reshape_reshape.6
  5.7 24.4 %all_to_all.35 = f32[64,2,12,1,96]{4,0,3,2,1:T(8,128)S(1)} all-to-all(f32[64,2,12,1,96]{4,0,3,2,1:T(8,128)S(1)} %copy.22), channel_id=1, replica_groups=mesh['grp'=2,'spec_0'=8,'spec_1'=8,'spec_2'=2] {'spec_2'}, dimensions={1} | all-to-all | bytes 1179648 | tf_op jit(solution)/shard_map/all_to_all | solution.py:33
  30.2 1.5 %copy.23 = f32[64,2,12,1,96]{4,1,3,2,0:T(2,128)} copy(f32[64,2,12,1,96]{4,0,3,2,1:T(8,128)S(1)} %all_to_all.35) | data formatting | bytes 1179648 | tf_op jit(solution)/shard_map/all_to_all | solution.py:33
  31.6 6.5 %all-to-all-start.1 = ((f32[64,2,12,1,96]{4,1,3,2,0:T(2,128)}), f32[64,2,12,1,96]{4,1,3,2,0:T(2,128)S(1)}, u32[]{:S(2)}, u32[]{:S(2)}) async-start(f32[64,2,12,1,96]{4,1,3,2,0:T(2,128)} %copy.23), calls=%async_computation.1 | async-start | bytes 1572864 | tf_op jit(solution)/shard_map/all_to_all | solution.py:33
  38.2 0.8 dynamic_slice.9
  38.9 0.8 dynamic_slice.10
  40.0 0.5 copy.25
  40.7 18.7 %all-to-all-done.1 = f32[64,2,12,1,96]{4,1,3,2,0:T(2,128)S(1)} async-done(((f32[64,2,12,1,96]{4,1,3,2,0:T(2,128)}), f32[64,2,12,1,96]{4,1,3,2,0:T(2,128)S(1)}, u32[]{:S(2)}, u32[]{:S(2)}) %all-to-all-start.1) | async-done | bytes 589856 | tf_op jit(solution)/shard_map/all_to_all | solution.py:33
  60.1 0.8 subtract_multiply_fusion.1
  61.5 1.0 fusion.24
  62.6 1.9 %fusion.26 = (f32[96]{0:T(128)S(1)}, f32[48,32,96]{2,1,0:T(8,128)}) fusion(f32[48,29,96]{2,1,0:T(8,128)S(1)} %pad_slice_fusion, f32[48,3,96]{2,1,0:T(4,128)S(1)} %pad_slice_fusion.1, f32[48,1,96]{2,1,0:T(1,128)S(1)} %pad_slice_fusion.4, f32[48,31,96]{2,1,0:T(8,128)S(1)} %pad_slice_fusion.5, f32[48,32,96]{2,1,0:T(8,128)S(1)} %get-tuple-element.10, ...), kind=kLoop, calls=%fused_computation.75 | loop fusion | flops 3096480 | bytes 4768320 | tf_op jit(solution)/shard_map/reduce_sum | solution.py:112
  64.5 1.2 fusion.25
  65.7 0.7 add.195
  66.4 22.6 %all_to_all.36 = f32[128,1,1]{2,1,0:T(1,128)S(1)} all-to-all(f32[128,1,1]{2,1,0:T(1,128)S(1)} %add.195), channel_id=1, replica_groups=mesh['grp'=2,'spec_0'=8,'spec_1'=8,'spec_2'=2] {'spec_0','spec_1','spec_2'}, dimensions={0} | all-to-all | bytes 1024 | tf_op jit(solution)/shard_map/all_to_all | solution.py:146
  89.0 7.5 %all-to-all-start.2 = ((f32[1536,1,96]{2,1,0:T(1,128)}), f32[1536,1,96]{2,1,0:T(1,128)S(1)}, u32[]{:S(2)}, u32[]{:S(2)}) async-start(f32[1536,1,96]{2,1,0:T(1,128)} %bitcast.3), calls=%async_computation.2 | async-start | bytes 1572864 | tf_op jit(solution)/shard_map/all_to_all | solution.py:143
  96.5 0.7 reduce_sum.49
  97.9 23.2 %all-to-all-done.2 = f32[1536,1,96]{2,1,0:T(1,128)S(1)} async-done(((f32[1536,1,96]{2,1,0:T(1,128)}), f32[1536,1,96]{2,1,0:T(1,128)S(1)}, u32[]{:S(2)}, u32[]{:S(2)}) %all-to-all-start.2) | async-done | bytes 589856 | tf_op jit(solution)/shard_map/all_to_all | solution.py:143
  121.2 1.3 %reshape.284 = f32[12,12288]{1,0:T(8,128)} reshape(f32[12,128,1,96]{3,1,0,2:T(8,128)S(1)} %copy.27) | data formatting | bytes 1179648 | tf_op jit(solution)/shard_map/reshape | solution.py:148
  (41 shorter events, 2.7 us)
Async XLA Ops:
  31.6 27.8 %all-to-all-start.1 = ((f32[64,2,12,1,96]{4,1,3,2,0:T(2,128)}), f32[64,2,12,1,96]{4,1,3,2,0:T(2,128)S(1)}, u32[]{:S(2)}, u32[]{:S(2)}) async-start(f32[64,2,12,1,96]{4,1,3,2,0:T(2,128)} %copy.23), calls=%async_computation.1 | async-start | bytes 1572864 | tf_op jit(solution)/shard_map/all_to_all | solution.py:33
  89.0 32.2 %all-to-all-start.2 = ((f32[1536,1,96]{2,1,0:T(1,128)}), f32[1536,1,96]{2,1,0:T(1,128)S(1)}, u32[]{:S(2)}, u32[]{:S(2)}) async-start(f32[1536,1,96]{2,1,0:T(1,128)} %bitcast.3), calls=%async_computation.2 | async-start | bytes 1572864 | tf_op jit(solution)/shard_map/all_to_all | solution.py:143
where the time goes:
time: 124 us
  blocking collectives  47 us (38%)
  waiting for transfers between devices  41.9 us (34%)
  starting transfers between devices  14 us (11%)
  other arithmetic  9.6 us (8%)
  local copies, waits for them, and re-layouts  8.38 us (7%)
  between operations  2.71 us (2%)
    all_to_all x1, blocking collectives, turned_blocks(): lax.all_to_all(pieces, axes[k], split_axis=k, concat_axis=k, tiled=True)  24.4 us
    all_to_all x1, waiting for transfers between devices, local(): lax.all_to_all(updated.reshape(NF * ND, 1, points), SPEC, split_axis=0, c...  23.2 us
    all_to_all x1, blocking collectives, local(): lax.all_to_all(own_total, SPEC, split_axis=0, concat_axis=1, tiled=True)  22.6 us
    all_to_all x1, waiting for transfers between devices, turned_blocks(): lax.all_to_all(pieces, axes[k], split_axis=k, concat_axis=k, tiled=True)  18.7 us
    all_to_all x1, starting transfers between devices, local(): lax.all_to_all(updated.reshape(NF * ND, 1, points), SPEC, split_axis=0, c...  7.53 us
    all_to_all x1, starting transfers between devices, turned_blocks(): lax.all_to_all(pieces, axes[k], split_axis=k, concat_axis=k, tiled=True)  6.5 us
  transfers between devices with their start and end apart: 2, of which 2 were waited for; matrix products, arithmetic and copies ran while one was open for 3% of the time, Pallas kernels for 0%

commit v1 on v0

v1 whole, which is shorter than its diff:
```python
import functools
import math

import jax
import jax.numpy as jnp
import numpy as np
from jax import lax
from jax.experimental import pallas as pl
from jax.experimental.pallas import tpu as pltpu
from jax.sharding import PartitionSpec as P

NF = 48
ND = 32
NLON = 384
SUBSTEPS = 2
SEA_DEV = 64
MESH = pl.DeviceIdType.MESH
LOG_RATIO = math.log(1.1)


def peer_order(side, cores):
    hops = lambda d: min(d, side - d)
    sign = lambda d: 0 if d == 0 else (1 if d <= side // 2 else -1)
    offsets = [(x, y, c) for x in range(side) for y in range(side) for c in range(cores)][1:]
    offsets.sort(key=lambda o: (-(hops(o[0]) + hops(o[1])), o[0] * 3 + o[1] * 5, o[2]))
    classes = {}
    for o in offsets:
        classes.setdefault((sign(o[0]), sign(o[1])), []).append(o)
    placed = []
    for members in classes.values():
        placed += [((i + 0.5) / len(members), o) for i, o in enumerate(members)]
    placed.sort(key=lambda item: item[0])
    return [o for _, o in placed]


def step_kernel(
    n, side, cores, order,
    x, mask2d, speed2d, angle2d,
    out, height_out, mean_out,
    field_a, field_b, stage, shifts, go_left, go_right, hist,
    send, recv, back, home, flat, rolled, updated, heights,
    send_sem, recv_sem,
):
    bins_dev, cells = x.shape
    half = bins_dev // 2
    chunks = cells // 128
    per_row = NLON // 128
    lat_count = cells // NLON
    sea_chunks = n * SEA_DEV // 128
    me = lax.axis_index("spec")
    my_x, my_y, my_c = me // (side * cores), lax.rem(me // cores, side), lax.rem(me, cores)

    def peer(o):
        return (
            lax.rem(my_x + o[0], side) * side + lax.rem(my_y + o[1], side)
        ) * cores + lax.rem(my_c + o[2], cores)

    barrier = pltpu.get_barrier_semaphore()
    for o in order:
        pl.semaphore_signal(barrier, inc=1, device_id={"spec": peer(o)}, device_id_type=MESH)

    lane = lax.broadcasted_iota(jnp.int32, (8, 128), 1)
    row = lax.broadcasted_iota(jnp.int32, (8, 128), 0)
    low = lane < SEA_DEV

    bits = (chunks * 128).bit_length() - 1
    land = (1 - mask2d[...]).astype(jnp.bfloat16)
    before = (
        lax.broadcasted_iota(jnp.int32, (128, 128), 0) < lax.broadcasted_iota(jnp.int32, (128, 128), 1)
    ).astype(jnp.bfloat16)
    above = (
        lax.broadcasted_iota(jnp.int32, (chunks, chunks), 1)
        < lax.broadcasted_iota(jnp.int32, (chunks, chunks), 0)
    ).astype(jnp.bfloat16)
    within = jnp.dot(land, before, preferred_element_type=jnp.float32)
    rows_above = jnp.dot(above, land, preferred_element_type=jnp.float32)
    count = within + jnp.dot(
        rows_above.astype(jnp.bfloat16),
        jnp.ones((128, 128), jnp.bfloat16),
        preferred_element_type=jnp.float32,
    )
    left = jnp.where(mask2d[...] != 0, count.astype(jnp.int32), 0)
    shifts[chunks:, :] = jnp.zeros((shifts.shape[0] - chunks, 128), jnp.int32)
    wide_lane = lax.broadcasted_iota(jnp.int32, (chunks, 128), 1)
    steps = 13
    for i in range(steps):
        d = 1 << i
        shifts[0:chunks, :] = left
        if d < 128:
            near = pltpu.roll(left, 128 - d, 1)
            far = pltpu.roll(shifts[1 : chunks + 1, :], 128 - d, 1)
            incoming = jnp.where(wide_lane < 128 - d, near, far)
        else:
            incoming = shifts[d // 128 : chunks + d // 128, :]
        goes = jnp.bitwise_and(left, d)
        comes = jnp.bitwise_and(incoming, d)
        go_right[i] = goes
        go_left[i] = comes
        left = jnp.where(comes != 0, incoming, jnp.where(goes != 0, 0, left))

    zero = jnp.zeros((8, 128), jnp.float32)
    pad = per_row
    for t in range(2):
        for v in range(pad):
            for f in (field_a, field_b):
                f[t, v] = zero
                f[t, pad + chunks + v] = zero
    for v in range(chunks):
        sea = mask2d[v : v + 1, :].astype(jnp.float32)
        stage[v, 0:bins_dev, :] = x[:, v * 128 : (v + 1) * 128] * sea
        for t in range(2):
            field_a[t, pad + v, 0:half, :] = stage[v, pl.ds(t, half, stride=2), :]

    freq, cw, ce, cs, cn = [], [], [], [], []
    for t in range(2):
        bin_ids = me * bins_dev + jnp.minimum(2 * row + t, bins_dev - 1)
        k = (bin_ids // ND).astype(jnp.float32)
        j = lax.rem(bin_ids, ND).astype(jnp.float32)
        pace = 0.2 * jnp.exp(-LOG_RATIO * k)
        heading = (2.0 * math.pi / ND) * (j + 0.5)
        ax, ay = pace * jnp.cos(heading), pace * jnp.sin(heading)
        cw.append(jnp.maximum(ax, 0.0))
        ce.append(-jnp.minimum(ax, 0.0))
        cs.append(jnp.maximum(ay, 0.0))
        cn.append(-jnp.minimum(ay, 0.0))
    for s in range(SUBSTEPS):
        src, dst = (field_a, field_b) if s % 2 == 0 else (field_b, field_a)
        for r in range(lat_count):
            latitude = math.radians(-75.0 + 150.0 * (r + 0.5) / lat_count)
            widen = float(1.0 / math.cos(latitude))
            for t in range(2):
                west_c, east_c = cw[t] * widen, ce[t] * widen
                own_c = 1.0 - west_c - east_c - cs[t] - cn[t]
                first = pad + r * per_row
                e = [src[t, first + q] for q in range(per_row)]
                right = [pltpu.roll(a, 1, 1) for a in e]
                leftw = [pltpu.roll(a, 127, 1) for a in e]
                for q in range(per_row):
                    west = jnp.where(lane == 0, right[q - 1], right[q])
                    east = jnp.where(lane == 127, leftw[(q + 1) % per_row], leftw[q])
                    new = (
                        own_c * e[q] + west_c * west + east_c * east
                        + cs[t] * src[t, first + q - per_row]
                        + cn[t] * src[t, first + q + per_row]
                    )
                    v = first + q - pad
                    if s < SUBSTEPS - 1:
                        new = new * mask2d[v : v + 1, :].astype(jnp.float32)
                    dst[t, first + q] = new
                    if s == SUBSTEPS - 1:
                        dst[t, first + q, half : half + 1, :] = (speed2d, angle2d)[t][v : v + 1, :]
    final = field_a if SUBSTEPS % 2 == 0 else field_b

    lane_steps = 7
    ready = {}
    turned = [[zero] * lane_steps for _ in range(2)]
    held = [[{} for _ in range(steps)] for _ in range(2)]
    for v in range(chunks - 1, -1, -1):
        moves = [go_left[i, v : v + 1, :] != 0 for i in range(lane_steps)]
        cur = []
        for t in range(2):
            a = final[t, pad + v]
            for i in range(lane_steps):
                d = 1 << i
                rot = pltpu.roll(a, 128 - d, 1)
                b = jnp.where(lane < 128 - d, rot, turned[t][i])
                turned[t][i] = rot
                a = jnp.where(jnp.broadcast_to(moves[i], (8, 128)), b, a)
            cur.append(a)
        for i in range(lane_steps, steps):
            dv = 1 << (i - 7)
            slot = i - lane_steps
            for t in range(2):
                a = cur[t]
                if dv <= 4:
                    held[t][i][v] = a
                else:
                    hist[slot, t, v] = a
                if v + dv < chunks and (v < sea_chunks or i < steps - 1):
                    older = held[t][i].pop(v + dv) if dv <= 4 else hist[slot, t, v + dv]
                    m = jnp.broadcast_to(go_left[i, v : v + 1, :] != 0, (8, 128))
                    cur[t] = jnp.where(m, older, a)
        if v < sea_chunks:
            even, odd = cur
            send[2 * v] = jnp.where(low, even, pltpu.roll(odd, 64, 1))
            send[2 * v + 1] = jnp.where(low, pltpu.roll(even, 64, 1), odd)

    pl.semaphore_wait(barrier, n - 1)

    def exchange(src, dst, rows, k):
        for o in order:
            to = peer(o)
            pltpu.make_async_remote_copy(
                src_ref=src.at[to, pl.ds(0, rows)],
                dst_ref=dst.at[me, pl.ds(0, rows)],
                send_sem=send_sem.at[k],
                recv_sem=recv_sem.at[k],
                device_id={"spec": to},
                device_id_type=MESH,
            ).start()
        dst[me] = src[me]

    def finish(ref, rows, sem):
        part = ref.at[pl.ds(0, n - 1), pl.ds(0, rows)]
        pltpu.make_async_copy(part, part, sem).wait()

    exchange(send, recv, half, 0)

    wind = send[me][half : half + 1, :]
    other = pltpu.roll(wind, 64, 1)
    lower = low[0:1, :]
    speed = jnp.where(lower, wind, other)
    angle = jnp.where(lower, other, wind)
    pair = lax.broadcasted_iota(jnp.int32, (ND // 2, 128), 0)
    side_id = (lax.broadcasted_iota(jnp.int32, (ND // 2, 128), 1) >= SEA_DEV).astype(jnp.int32)
    low16 = side_id == 0
    dirs = (2.0 * math.pi / ND) * ((2 * pair + side_id).astype(jnp.float32) + 0.5)
    toward = speed * (jnp.cos(dirs) * jnp.cos(angle) + jnp.sin(dirs) * jnp.sin(angle))

    finish(recv, half, recv_sem.at[0])

    for p in range(n):
        flat[half * p : half * p + half, :] = recv[p, 0:half, :]

    rows_k = ND // 2

    def turns(a, amounts):
        s = pltpu.roll(a, 64, 1)
        need = {1: (1, 0), -1: (0, -1), 3: (2, 1), -3: (-1, -2)}
        by = {0: s}
        for m in amounts:
            for w in need[m]:
                if w not in by:
                    by[w] = pltpu.roll(s, w % rows_k, 0)
        return [jnp.where(low16, by[need[m][0]], by[need[m][1]]) for m in amounts]

    omega = [float(math.exp(LOG_RATIO * (k - NF // 2))) for k in range(NF)]
    m0 = m1 = None
    for k in range(NF):
        a = flat[rows_k * k : rows_k * (k + 1), :]
        m0 = a if k == 0 else m0 + a
        m1 = omega[k] * a if k == 0 else m1 + omega[k] * a
        for w, b in enumerate(turns(a, (1, -1, 3, -3))):
            rolled[w, rows_k * k : rows_k * (k + 1), :] = b

    def over_bins(a):
        a = jnp.sum(a, axis=0, keepdims=True)
        return (a + pltpu.roll(a, 64, 1)) * (1.0 / (NF * ND))

    m0, m1 = over_bins(m0), over_bins(m1)
    mean_freq = m1 / (m0 + 1e-6)
    steep = m0 * mean_freq * mean_freq
    breaking = steep * steep / (1.0 + steep * steep)

    own, from_low, total = {}, {}, None
    for k in range(NF + 3):
        from_high = None
        if 3 <= k <= NF - 3:
            a = flat[rows_k * k : rows_k * (k + 1), :]
            get = lambda w, kk: rolled[w, rows_k * kk : rows_k * (kk + 1), :]
            rates = []
            for plus, minus in ((get(1, k + 2), get(2, k - 3)), (get(0, k + 2), get(3, k - 3))):
                rates.append(0.001 * a * (a * (plus + minus) - 2.0 * plus * minus))
            up, down = turns(rates[0], (1, -3)), turns(rates[1], (-1, 3))
            own[k] = -2.0 * (rates[0] + rates[1])
            from_low[k + 2] = up[0] + down[0]
            from_high = up[1] + down[1]
        f = k - 3
        if f < 0:
            continue
        a = flat[rows_k * f : rows_k * (f + 1), :]
        gain = (0.05 * omega[f]) * jnp.maximum(0.0, omega[f] * toward - 1.0)
        new = a + (gain - (0.03 * omega[f]) * breaking) * a
        for part in (own.pop(f, None), from_low.pop(f, None), from_high):
            if part is not None:
                new = new + part
        updated[rows_k * f : rows_k * (f + 1), :] = new
        total = new if total is None else total + new
    height = 4.0 * jnp.sqrt(over_bins(total) + 1e-6)

    for p in range(n):
        back[p, half : half + 1, :] = height
        back[p, 0:half, :] = updated[half * p : half * p + half, :]

    exchange(back, home, half + 1, 1)
    finish(send, half, send_sem.at[0])
    finish(home, half + 1, recv_sem.at[1])

    turned = [[zero] * lane_steps for _ in range(2)]
    held = [[{} for _ in range(steps)] for _ in range(2)]
    height_sum = zero
    for v in range(chunks):
        if v < sea_chunks:
            a, b = home[2 * v], home[2 * v + 1]
            cur = [jnp.where(low, a, pltpu.roll(b, 64, 1)), jnp.where(low, pltpu.roll(a, 64, 1), b)]
            height_sum = height_sum + cur[0]
        else:
            cur = [zero, zero]
        for i in range(steps - 1, lane_steps - 1, -1):
            dv = 1 << (i - 7)
            slot = i - lane_steps
            for t in range(2):
                a = cur[t]
                if dv <= 4:
                    held[t][i][v] = a
                else:
                    hist[slot, t, v] = a
                if v >= dv:
                    older = held[t][i].pop(v - dv) if dv <= 4 else hist[slot, t, v - dv]
                    m = jnp.broadcast_to(go_right[i, v : v + 1, :] != 0, (8, 128))
                    cur[t] = jnp.where(m, older, a)
        sea = jnp.broadcast_to(mask2d[v : v + 1, :] != 0, (8, 128))
        for t in range(2):
            a = cur[t]
            for i in range(lane_steps - 1, -1, -1):
                d = 1 << i
                rot = pltpu.roll(a, d, 1)
                b = jnp.where(lane < d, turned[t][i], rot)
                turned[t][i] = rot
                m = jnp.broadcast_to(go_right[i, v : v + 1, :] != 0, (8, 128))
                a = jnp.where(m, b, a)
            a = jnp.where(sea, a, 0.0)
            stage[v, pl.ds(t, half, stride=2), :] = a[0:half]
            if t == 0:
                heights[v : v + 1, :] = a[half : half + 1]
        out[:, v * 128 : (v + 1) * 128] = stage[v, 0:bins_dev, :]

    points = cells // n
    group = 128 * 3 // points
    start = me // group * 3
    three = [heights[pl.ds(start + q, 1), :] for q in range(3)]
    u = lax.rem(me, group)
    picked = None
    for g in range(group):
        first, offset = g * points // 128, g * points % 128
        piece = three[first]
        if offset:
            nxt = three[min(first + 1, 2)]
            piece = jnp.where(
                lane[0:1] < 128 - offset, pltpu.roll(piece, 128 - offset, 1), pltpu.roll(nxt, 128 - offset, 1)
            )
        picked = piece if picked is None else jnp.where(u == g, piece, picked)
    height_out[...] = picked[:, 0:points]
    mean_out[...] = jnp.sum(height_sum[half : half + 1, :], axis=1, keepdims=True) * (1.0 / (SEA_DEV * n))
    finish(back, half + 1, send_sem.at[1])


def solution(mesh):
    n = mesh.shape["spec"]
    cores = 2
    side = math.isqrt(n // cores)
    order = peer_order(side, cores)

    def local(spectrum, sea_mask, wind_speed, wind_angle):
        bins_dev, cells = spectrum.shape
        chunks = cells // 128
        per_row = NLON // 128
        padded = chunks + 2 * per_row
        vmem = pl.BlockSpec(memory_space=pltpu.VMEM)
        new_spectrum, height, mean = pl.pallas_call(
            functools.partial(step_kernel, n, side, cores, order),
            name="wave_step",
            out_shape=(
                jax.ShapeDtypeStruct((bins_dev, cells), jnp.float32),
                jax.ShapeDtypeStruct((1, cells // n), jnp.float32),
                jax.ShapeDtypeStruct((1, 1), jnp.float32),
            ),
            in_specs=[vmem] * 4,
            out_specs=(vmem,) * 3,
            scratch_shapes=[
                pltpu.VMEM((2, padded, 8, 128), jnp.float32),
                pltpu.VMEM((2, padded, 8, 128), jnp.float32),
                pltpu.VMEM((chunks, 16, 128), jnp.float32),
                pltpu.VMEM((chunks + 32, 128), jnp.int32),
                pltpu.VMEM((13, chunks, 128), jnp.int32),
                pltpu.VMEM((13, chunks, 128), jnp.int32),
                pltpu.VMEM((6, 2, chunks, 8, 128), jnp.float32),
                pltpu.VMEM((n, 8, 128), jnp.float32),
                pltpu.VMEM((n, 8, 128), jnp.float32),
                pltpu.VMEM((n, 8, 128), jnp.float32),
                pltpu.VMEM((n, 8, 128), jnp.float32),
                pltpu.VMEM((NF * ND // 2, 128), jnp.float32),
                pltpu.VMEM((4, NF * ND // 2, 128), jnp.float32),
                pltpu.VMEM((NF * ND // 2, 128), jnp.float32),
                pltpu.VMEM((chunks, 128), jnp.float32),
                pltpu.SemaphoreType.DMA((2,)),
                pltpu.SemaphoreType.DMA((2,)),
            ],
            compiler_params=pltpu.CompilerParams(collective_id=0, has_side_effects=True),
        )(
            spectrum,
            sea_mask.reshape(chunks, 128),
            wind_speed.reshape(chunks, 128),
            wind_angle.reshape(chunks, 128),
        )
        return new_spectrum, height.reshape(-1), mean.reshape(1)

    return jax.shard_map(
        local,
        mesh=mesh,
        in_specs=(P(("grp", "spec"), None), P(), P("grp"), P("grp")),
        out_specs=(P(("grp", "spec"), None), P(("grp", "spec")), P("grp")),
        check_vma=False,
    )
```

time: 124 us -> 154 us (1.24)
  Pallas kernels: 0 us -> 149 us
  blocking collectives: 47 us -> 0 us
  waiting for transfers between devices: 41.9 us -> 0 us
  starting transfers between devices: 14 us -> 0 us
  other arithmetic: 9.6 us -> 0 us
  local copies, waits for them, and re-layouts: 8.38 us -> 2.58 us
    pallas_call x0 -> x1, Pallas kernels: none -> 149 us  [local(): pl.pallas_call(functools.partial(step_kernel, n, side, cores, order), nam...]
    all_to_all x2 -> x0, blocking collectives: 47 us -> none  [the longest x1 24.4 us: turned_blocks(): lax.all_to_all(pieces, axes[k], split_axis=k, concat_axis=k, tiled=True)]
    all_to_all x2 -> x0, waiting for transfers between devices: 41.9 us -> none  [the longest x1 23.2 us: local(): lax.all_to_all(updated.reshape(NF * ND, 1, points), SPEC, split_axis=0, c...]
    all_to_all x2 -> x0, starting transfers between devices: 14 us -> none  [the longest x1 7.53 us: local(): lax.all_to_all(updated.reshape(NF * ND, 1, points), SPEC, split_axis=0, c...]
    reduce_sum x4 -> x0, other arithmetic: 4.78 us -> none  [the longest x1 1.86 us: source_terms(): raw_height = 4.0 * jnp.sqrt(jnp.mean(updated, axis=(0, 1)) + 1e-06)]
    mul x10 -> x0, other arithmetic: 3.66 us -> none  [the longest x2 1.47 us: upwind_step(): return updated * sea_grid]
    unnamed x1 -> x4, local copies, waits for them, and re-layouts: 0.15 us -> 2.58 us
    slice x22 -> x0, local copies, waits for them, and re-layouts: 1.84 us -> none  [the longest x4 0.68 us: upwind_step(): east_cell = jnp.roll(energy, -1, axis=2)]
  transfers between devices with their start and end apart: 2 -> 0, of which waited for: 2 -> 0; matrix products, arithmetic and copies ran while one was open for 3% -> 0% of each run, Pallas kernels for 0% -> 0%
where the time goes in v1:
time: 154 us
  Pallas kernels  149 us (97%)
  local copies, waits for them, and re-layouts  2.58 us (2%)
  between operations  2.4 us (2%)
    pallas_call x1, Pallas kernels, local(): pl.pallas_call(functools.partial(step_kernel, n, side, cores, order), nam...  149 us

profile of v1, /device:TPU:513, one launch (start us, length us, event | category | flops | bytes accessed | tf_op | source)
XLA Modules:
  0.0 153.6 jit_solution(4180648943839742981)
XLA Ops:
  0.6 148.6 %wave_step.1 = (f32[12,12288]{1,0:T(8,128)}, f32[1,96]{1,0:T(1,128)}, f32[1,1]{1,0:T(1,128)}) custom-call(f32[12,12288]{1,0:T(8,128)} %x.1, s32[96,128]{1,0:T(8,128)} %bitcast.5, f32[96,128]{1,0:T(8,128)} %bitcast.6, f32[96,128]{1,0:T(8,128)} %bitcast.7), custom_call_target="tpu_custom_call" | custom-call | tf_op jit(solution)/shard_map/wave_step/pallas_call | solution.py:360
  149.2 0.0 copy-start
  149.2 2.1 %copy.10 = f32[12,12288]{1,0:T(8,128)} copy(f32[12,12288]{1,0:T(8,128)} %get-tuple-element.12) | data formatting | bytes 1179648
  151.3 0.0 copy-done
  151.3 0.5 copy.11
Async XLA Ops:
  149.2 2.1 %copy-start = (f32[1,96]{1,0:T(1,128)S(1)}, f32[1,96]{1,0:T(1,128)}, u32[]{:S(2)}) copy-start(f32[1,96]{1,0:T(1,128)} %get-tuple-element.7) | copy-start | bytes 1156

commit v2 on v1

v2 whole, which is shorter than its diff:
```python
import functools
import math

import jax
import jax.numpy as jnp
import numpy as np
from jax import lax
from jax.experimental import pallas as pl
from jax.experimental.pallas import tpu as pltpu
from jax.sharding import PartitionSpec as P

NF = 48
ND = 32
NLON = 384
SUBSTEPS = 2
SEA_DEV = 64
MESH = pl.DeviceIdType.MESH
LOG_RATIO = math.log(1.1)
PAIRS = ND // 2
LANE_STEPS = 7
STEPS = 13
REACH = 32


def tables(lat_count):
    heading = 2.0 * np.pi * (np.arange(ND) + 0.5) / ND
    wrapped = np.concatenate([heading, heading[:24]])
    flat = lambda a: np.repeat(np.asarray(a)[:, None], 128, 1)
    paired = np.repeat(heading.reshape(PAIRS, 2), SEA_DEV, axis=1)
    latitude = np.radians(-75.0 + 150.0 * (np.arange(lat_count) + 0.5) / lat_count)
    k = np.arange(NF)
    rows, at = [], {}
    for name, block in (
        ("cos", flat(np.cos(wrapped))),
        ("sin", flat(np.sin(wrapped))),
        ("pair_cos", np.cos(paired)),
        ("pair_sin", np.sin(paired)),
        ("widen", flat(1.0 / np.cos(latitude))),
        ("omega", flat(np.exp(LOG_RATIO * (k - NF // 2)))),
        ("rate", flat(np.where((k >= 3) & (k <= NF - 3), 0.001, 0.0))),
    ):
        at[name] = sum(len(r) for r in rows)
        rows.append(block)
    return np.concatenate(rows).astype(np.float32), at


def step_kernel(
    n, side, cores, at,
    x_hbm, mask2d, speed2d, angle2d, tab,
    out, height_out, mean_out,
    x, field_a, field_b, stage, shifts, go_left, go_right, hist,
    send, recv, back, home, flat, energy, rolled, own, low_part, high_part, heights,
    send_sem, recv_sem, load_sem,
):
    bins_dev, cells = x.shape
    half = bins_dev // 2
    chunks = cells // 128
    per_row = NLON // 128
    lat_count = cells // NLON
    me = lax.axis_index("spec")
    my_x, my_y, my_c = me // (side * cores), lax.rem(me // cores, side), lax.rem(me, cores)

    load = pltpu.make_async_copy(x_hbm, x, load_sem)
    load.start()

    def peers(act):
        def hop(u):
            return side // 2 + jnp.where(lax.rem(u, 2) == 0, u // 2, -((u + 1) // 2))

        def chip(s, u):
            px = lax.rem(my_x + hop(u), side)
            py = lax.rem(my_y + hop(s - u), side)
            first = (px * side + py) * cores
            act(first + my_c)
            for c in range(1, cores):
                act(first + lax.rem(my_c + c, cores))

        def diagonal(s, carry):
            def one(u, inner):
                chip(s, u)
                return inner

            return lax.fori_loop(jnp.maximum(0, s - side + 1), jnp.minimum(side - 1, s) + 1, one, carry)

        lax.fori_loop(0, 2 * side - 2, diagonal, 0)
        for c in range(1, cores):
            act(me - my_c + lax.rem(my_c + c, cores))

    barrier = pltpu.get_barrier_semaphore()
    peers(
        lambda to: pl.semaphore_signal(barrier, inc=1, device_id={"spec": to}, device_id_type=MESH)
    )

    lane = lax.broadcasted_iota(jnp.int32, (8, 128), 1)
    row = lax.broadcasted_iota(jnp.int32, (8, 128), 0)
    low = lane < SEA_DEV

    is_sea = mask2d[...] != 0
    land = jnp.where(is_sea, 0.0, 1.0).astype(jnp.bfloat16)
    before = (
        lax.broadcasted_iota(jnp.int32, (128, 128), 0) < lax.broadcasted_iota(jnp.int32, (128, 128), 1)
    ).astype(jnp.bfloat16)
    above = (
        lax.broadcasted_iota(jnp.int32, (chunks, chunks), 1)
        < lax.broadcasted_iota(jnp.int32, (chunks, chunks), 0)
    ).astype(jnp.bfloat16)
    rows_above = jnp.dot(above, land, preferred_element_type=jnp.float32)
    count = jnp.dot(land, before, preferred_element_type=jnp.float32) + jnp.dot(
        rows_above.astype(jnp.bfloat16),
        jnp.ones((128, 128), jnp.bfloat16),
        preferred_element_type=jnp.float32,
    )
    shifts[0:chunks, :] = jnp.where(is_sea, count.astype(jnp.int32), 0)
    shifts[chunks:, :] = jnp.zeros((shifts.shape[0] - chunks, 128), jnp.int32)
    go_left[...] = jnp.zeros_like(go_left)
    go_right[...] = jnp.zeros_like(go_right)
    wide_lane = lax.broadcasted_iota(jnp.int32, (chunks, 128), 1)

    def settle(left, incoming, d):
        goes = jnp.bitwise_and(left, d)
        comes = jnp.bitwise_and(incoming, d)
        go_right[...] += goes
        go_left[...] += comes
        shifts[0:chunks, :] = jnp.where(comes != 0, incoming, jnp.where(goes != 0, 0, left))

    def lane_step(i, carry):
        d = jnp.left_shift(1, i)
        left = shifts[0:chunks, :]
        near = pltpu.roll(left, 128 - d, 1)
        far = pltpu.roll(shifts[1 : chunks + 1, :], 128 - d, 1)
        settle(left, jnp.where(wide_lane < 128 - d, near, far), d)
        return carry

    lax.fori_loop(0, LANE_STEPS, lane_step, 0)
    for i in range(LANE_STEPS, STEPS):
        dv = 1 << (i - LANE_STEPS)
        settle(shifts[0:chunks, :], shifts[dv : chunks + dv, :], 1 << i)

    zero = jnp.zeros((8, 128), jnp.float32)
    pad = per_row
    for t in range(2):
        for v in range(pad):
            for f in (field_a, field_b):
                f[t, v] = zero
                f[t, pad + chunks + v] = zero
    base = (me * bins_dev) % ND
    cw, ce, cs, cn = [], [], [], []
    for t in range(2):
        k = ((me * bins_dev + jnp.minimum(2 * row + t, bins_dev - 1)) // ND).astype(jnp.float32)
        pace = 0.2 * jnp.exp(-LOG_RATIO * k)
        ax = pace * tab[pl.ds(at["cos"] + base + t, 8, stride=2), :]
        ay = pace * tab[pl.ds(at["sin"] + base + t, 8, stride=2), :]
        cw.append(jnp.maximum(ax, 0.0))
        ce.append(-jnp.minimum(ax, 0.0))
        cs.append(jnp.maximum(ay, 0.0))
        cn.append(-jnp.minimum(ay, 0.0))
    load.wait()

    def sea_row(v):
        return mask2d[pl.ds(v, 1), :] != 0

    def split_bins(g, carry):
        for u in range(8):
            v = g * 8 + u
            cols = pl.ds(pl.multiple_of(v * 128, 128), 128)
            stage[u, 0:bins_dev, :] = jnp.where(sea_row(v), x[:, cols], 0.0)
            for t in range(2):
                field_a[t, pad + v, 0:half, :] = stage[u, pl.ds(t, half, stride=2), :]
        return carry

    lax.fori_loop(0, chunks // 8, split_bins, 0)

    for s in range(SUBSTEPS):
        src, dst = (field_a, field_b) if s % 2 == 0 else (field_b, field_a)

        def advance(g, carry, src=src, dst=dst, s=s):
            for ru in range(2):
                r = g * 2 + ru
                widen = tab[pl.ds(at["widen"] + r, 1), :]
                first = pad + r * per_row
                for t in range(2):
                    west_c, east_c = cw[t] * widen, ce[t] * widen
                    own_c = 1.0 - west_c - east_c - cs[t] - cn[t]
                    e = [src[t, first + q] for q in range(per_row)]
                    right = [pltpu.roll(a, 1, 1) for a in e]
                    left = [pltpu.roll(a, 127, 1) for a in e]
                    for q in range(per_row):
                        west = jnp.where(lane == 0, right[q - 1], right[q])
                        east = jnp.where(lane == 127, left[(q + 1) % per_row], left[q])
                        new = (
                            own_c * e[q] + west_c * west + east_c * east
                            + cs[t] * src[t, first + q - per_row]
                            + cn[t] * src[t, first + q + per_row]
                        )
                        v = first + q - pad
                        if s < SUBSTEPS - 1:
                            dst[t, first + q] = jnp.where(sea_row(v), new, 0.0)
                        else:
                            wind = (speed2d, angle2d)[t][pl.ds(v, 1), :]
                            dst[t, first + q] = jnp.where(row == half, wind, new)
            return carry

        lax.fori_loop(0, lat_count // 2, advance, 0)
    final = field_a if SUBSTEPS % 2 == 0 else field_b

    unroll = 8

    def gather(g, carry):
        turned = list(carry)
        for u in range(unroll):
            v = chunks - 1 - (g * unroll + u)
            word = jnp.broadcast_to(go_left[pl.ds(v, 1), :], (8, 128))
            moves = [jnp.bitwise_and(word, 1 << i) != 0 for i in range(STEPS)]
            cur = []
            for t in range(2):
                a = final[t, pad + v]
                for i in range(LANE_STEPS):
                    d = 1 << i
                    rot = pltpu.roll(a, 128 - d, 1)
                    b = jnp.where(lane < 128 - d, rot, turned[t * LANE_STEPS + i])
                    turned[t * LANE_STEPS + i] = rot
                    a = jnp.where(moves[i], b, a)
                for i in range(LANE_STEPS, STEPS):
                    dv = 1 << (i - LANE_STEPS)
                    hist[i - LANE_STEPS, t, v] = a
                    a = jnp.where(moves[i], hist[i - LANE_STEPS, t, v + dv], a)
                cur.append(a)
            even, odd = cur
            send[2 * v] = jnp.where(low, even, pltpu.roll(odd, 64, 1))
            send[2 * v + 1] = jnp.where(low, pltpu.roll(even, 64, 1), odd)
        return tuple(turned)

    lax.fori_loop(0, chunks // unroll, gather, (zero,) * (2 * LANE_STEPS))

    pl.semaphore_wait(barrier, n - 1)

    def exchange(src, dst, rows, k):
        def push(to):
            pltpu.make_async_remote_copy(
                src_ref=src.at[to, pl.ds(0, rows)],
                dst_ref=dst.at[me, pl.ds(0, rows)],
                send_sem=send_sem.at[k],
                recv_sem=recv_sem.at[k],
                device_id={"spec": to},
                device_id_type=MESH,
            ).start()

        peers(push)
        dst[me] = src[me]

    def finish(ref, rows, sem):
        part = ref.at[pl.ds(0, n - 1), pl.ds(0, rows)]
        pltpu.make_async_copy(part, part, sem).wait()

    exchange(send, recv, half, 0)

    wind = send[me][half : half + 1, :]
    other = pltpu.roll(wind, SEA_DEV, 1)
    speed = jnp.where(low[0:1], wind, other)
    angle = jnp.where(low[0:1], other, wind)
    toward = speed * (
        tab[at["pair_cos"] : at["pair_cos"] + PAIRS, :] * jnp.cos(angle)
        + tab[at["pair_sin"] : at["pair_sin"] + PAIRS, :] * jnp.sin(angle)
    )
    low16 = lax.broadcasted_iota(jnp.int32, (PAIRS, 128), 1) < SEA_DEV
    zero16 = jnp.zeros((PAIRS, 128), jnp.float32)
    for w in range(4):
        for k in (0, 1, 2, NF + 3, NF + 4):
            rolled[w, k] = zero16
    for k in range(2):
        low_part[k] = zero16
    for k in range(3):
        high_part[NF + k] = zero16

    def turns(a, amounts):
        s = pltpu.roll(a, SEA_DEV, 1)
        need = {1: (1, 0), -1: (0, -1), 3: (2, 1), -3: (-1, -2)}
        by = {0: s}
        for m in amounts:
            for w in need[m]:
                if w not in by:
                    by[w] = pltpu.roll(s, w % PAIRS, 0)
        return [jnp.where(low16, by[need[m][0]], by[need[m][1]]) for m in amounts]

    group = 8
    per_group = half * group // PAIRS
    finish(recv, half, recv_sem.at[0])

    def arrange(g, carry):
        m0, m1 = carry
        for i in range(group):
            flat[g, half * i : half * i + half, :] = recv[g * group + i, 0:half, :]
        for q in range(per_group):
            k = g * per_group + q
            a = flat[g, PAIRS * q : PAIRS * (q + 1), :]
            energy[k] = a
            m0 = m0 + a
            m1 = m1 + tab[pl.ds(at["omega"] + k, 1), :] * a
            for w, b in enumerate(turns(a, (1, -1, 3, -3))):
                rolled[w, k + 3] = b
        return m0, m1

    m0, m1 = lax.fori_loop(0, n // group, arrange, (zero16, zero16))

    def over_bins(a):
        a = jnp.sum(a, axis=0, keepdims=True)
        return (a + pltpu.roll(a, SEA_DEV, 1)) * (1.0 / (NF * ND))

    m0, m1 = over_bins(m0), over_bins(m1)
    mean_freq = m1 / (m0 + 1e-6)
    steep = m0 * mean_freq * mean_freq
    breaking = steep * steep / (1.0 + steep * steep)

    def transfer(g, carry):
        for q in range(per_group):
            k = g * per_group + q
            a = energy[k]
            factor = tab[pl.ds(at["rate"] + k, 1), :] * a
            rates = []
            for plus, minus in ((rolled[1, k + 5], rolled[2, k]), (rolled[0, k + 5], rolled[3, k])):
                rates.append(factor * (a * (plus + minus) - 2.0 * plus * minus))
            up, down = turns(rates[0], (1, -3)), turns(rates[1], (-1, 3))
            own[k] = -2.0 * (rates[0] + rates[1])
            low_part[k + 2] = up[0] + down[0]
            high_part[k] = up[1] + down[1]
        return carry

    lax.fori_loop(0, n // group, transfer, 0)

    def renew(g, total):
        for q in range(per_group):
            k = g * per_group + q
            a = energy[k]
            omega = tab[pl.ds(at["omega"] + k, 1), :]
            gain = (0.05 * omega) * jnp.maximum(0.0, omega * toward - 1.0)
            new = a + (gain - (0.03 * omega) * breaking) * a
            new = new + own[k] + low_part[k] + high_part[k + 3]
            total = total + new
            flat[g, PAIRS * q : PAIRS * (q + 1), :] = new
        for i in range(group):
            back[g * group + i, 0:half, :] = flat[g, half * i : half * i + half, :]
        return total

    total = lax.fori_loop(0, n // group, renew, zero16)
    height = 4.0 * jnp.sqrt(over_bins(total) + 1e-6)

    def add_height(g, carry):
        for i in range(group):
            back[g * group + i, half : half + 1, :] = height
        return carry

    lax.fori_loop(0, n // group, add_height, 0)

    exchange(back, home, half + 1, 1)
    finish(send, half, send_sem.at[0])
    finish(home, half + 1, recv_sem.at[1])

    def scatter(g, carry):
        turned = list(carry)
        for u in range(unroll):
            v = g * unroll + u
            word = jnp.broadcast_to(go_right[pl.ds(v, 1), :], (8, 128))
            moves = [jnp.bitwise_and(word, 1 << i) != 0 for i in range(STEPS)]
            sea = jnp.broadcast_to(mask2d[pl.ds(v, 1), :], (8, 128)) != 0
            a, b = home[2 * v], home[2 * v + 1]
            cur = [
                jnp.where(low, a, pltpu.roll(b, SEA_DEV, 1)),
                jnp.where(low, pltpu.roll(a, SEA_DEV, 1), b),
            ]
            for t in range(2):
                a = cur[t]
                for i in range(STEPS - 1, LANE_STEPS - 1, -1):
                    dv = 1 << (i - LANE_STEPS)
                    hist[i - LANE_STEPS, t, REACH + v] = a
                    a = jnp.where(moves[i], hist[i - LANE_STEPS, t, REACH + v - dv], a)
                for i in range(LANE_STEPS - 1, -1, -1):
                    d = 1 << i
                    rot = pltpu.roll(a, d, 1)
                    b = jnp.where(lane < d, turned[t * LANE_STEPS + i], rot)
                    turned[t * LANE_STEPS + i] = rot
                    a = jnp.where(moves[i], b, a)
                a = jnp.where(sea, a, 0.0)
                stage[u, pl.ds(t, half, stride=2), :] = a[0:half]
                if t == 0:
                    heights[pl.ds(v, 1), :] = a[half : half + 1]
            out[:, pl.ds(pl.multiple_of(v * 128, 128), 128)] = stage[u, 0:bins_dev, :]
        return tuple(turned)

    lax.fori_loop(0, chunks // unroll, scatter, (zero,) * (2 * LANE_STEPS))

    points = cells // n
    together = NLON // points
    start = me // together * per_row
    three = [heights[pl.ds(start + q, 1), :] for q in range(per_row)]
    u = lax.rem(me, together)
    picked = None
    for g in range(together):
        first, offset = g * points // 128, g * points % 128
        piece = three[first]
        if offset:
            after = three[min(first + 1, per_row - 1)]
            piece = jnp.where(
                lane[0:1] < 128 - offset,
                pltpu.roll(piece, 128 - offset, 1),
                pltpu.roll(after, 128 - offset, 1),
            )
        picked = piece if picked is None else jnp.where(u == g, piece, picked)
    height_out[...] = picked[:, 0:points]
    all_heights = jnp.sum(heights[...], axis=0, keepdims=True)
    mean_out[...] = jnp.sum(all_heights, axis=1, keepdims=True) * (1.0 / (SEA_DEV * n))
    finish(back, half + 1, send_sem.at[1])


def solution(mesh):
    n = mesh.shape["spec"]
    cores = 2
    side = math.isqrt(n // cores)

    def local(spectrum, sea_mask, wind_speed, wind_angle):
        bins_dev, cells = spectrum.shape
        chunks = cells // 128
        padded = chunks + 2 * (NLON // 128)
        tab, at = tables(cells // NLON)
        vmem = pl.BlockSpec(memory_space=pltpu.VMEM)
        words = pltpu.VMEM((chunks, 128), jnp.int32)
        by_freq = lambda *dims: pltpu.VMEM((*dims, PAIRS, 128), jnp.float32)
        messages = lambda count: pltpu.VMEM((count, 8, 128), jnp.float32)
        new_spectrum, height, mean = pl.pallas_call(
            functools.partial(step_kernel, n, side, cores, at),
            name="wave_step",
            out_shape=(
                jax.ShapeDtypeStruct((bins_dev, cells), jnp.float32),
                jax.ShapeDtypeStruct((1, cells // n), jnp.float32),
                jax.ShapeDtypeStruct((1, 1), jnp.float32),
            ),
            in_specs=[pl.BlockSpec(memory_space=pl.ANY)] + [vmem] * 4,
            out_specs=(vmem,) * 3,
            scratch_shapes=[
                pltpu.VMEM((bins_dev, cells), jnp.float32),
                pltpu.VMEM((2, padded, 8, 128), jnp.float32),
                pltpu.VMEM((2, padded, 8, 128), jnp.float32),
                pltpu.VMEM((8, 16, 128), jnp.float32),
                pltpu.VMEM((chunks + REACH, 128), jnp.int32),
                words,
                words,
                pltpu.VMEM((STEPS - LANE_STEPS, 2, chunks + REACH, 8, 128), jnp.float32),
                messages(2 * chunks),
                messages(n),
                messages(n),
                messages(2 * chunks),
                pltpu.VMEM((n // 8, 8 * bins_dev // 2, 128), jnp.float32),
                by_freq(NF),
                by_freq(4, NF + 5),
                by_freq(NF),
                by_freq(NF + 2),
                by_freq(NF + 3),
                pltpu.VMEM((chunks, 128), jnp.float32),
                pltpu.SemaphoreType.DMA((2,)),
                pltpu.SemaphoreType.DMA((2,)),
                pltpu.SemaphoreType.DMA,
            ],
            compiler_params=pltpu.CompilerParams(collective_id=0, has_side_effects=True),
        )(
            spectrum,
            sea_mask.reshape(chunks, 128),
            wind_speed.reshape(chunks, 128),
            wind_angle.reshape(chunks, 128),
            tab,
        )
        return new_spectrum, height.reshape(-1), mean.reshape(1)

    return jax.shard_map(
        local,
        mesh=mesh,
        in_specs=(P(("grp", "spec"), None), P(), P("grp"), P("grp")),
        out_specs=(P(("grp", "spec"), None), P(("grp", "spec")), P("grp")),
        check_vma=False,
    )
```

time: 154 us -> 84.5 us (0.55)
  Pallas kernels: 149 us -> 79.3 us
    pallas_call x1, Pallas kernels: 149 us -> 79.3 us  [local(): pl.pallas_call(functools.partial(step_kernel, n, side, cores, at), name='...]
where the time goes in v2:
time: 84.5 us; the launch traced here: 84.3 us
  Pallas kernels  79.3 us (94%)
  local copies, waits for them, and re-layouts  2.58 us (3%)
  between operations  2.4 us (3%)
    pallas_call x1, Pallas kernels, local(): pl.pallas_call(functools.partial(step_kernel, n, side, cores, at), name='...  79.3 us
    unnamed x4, local copies, waits for them, and re-layouts  2.58 us

profile of v2, /device:TPU:513, one launch (start us, length us, event | category | flops | bytes accessed | tf_op | source)
XLA Modules:
  0.0 84.3 jit_solution(14666653537042099606)
XLA Ops:
  0.6 79.3 %wave_step.1 = (f32[12,12288]{1,0:T(8,128)}, f32[1,96]{1,0:T(1,128)}, f32[1,1]{1,0:T(1,128)}) custom-call(f32[12,12288]{1,0:T(8,128)} %x_hbm.1, s32[96,128]{1,0:T(8,128)} %bitcast.5, f32[96,128]{1,0:T(8,128)} %bitcast.6, f32[96,128]{1,0:T(8,128)} %bitcast.7, f32[272,128]{1,0:T(8,128)} %constant.2.clone.tab), custom_call_target="tpu_custom_call" | custom-call | tf_op jit(solution)/shard_map/wave_step/pallas_call | solution.py:428
  80.0 0.0 copy-start
  80.0 2.1 %copy.11 = f32[12,12288]{1,0:T(8,128)} copy(f32[12,12288]{1,0:T(8,128)} %get-tuple-element.12) | data formatting | bytes 1179648
  82.0 0.0 copy-done
  82.1 0.5 copy.12
Async XLA Ops:
  80.0 2.1 %copy-start = (f32[1,96]{1,0:T(1,128)S(1)}, f32[1,96]{1,0:T(1,128)}, u32[]{:S(2)}) copy-start(f32[1,96]{1,0:T(1,128)} %get-tuple-element.7) | copy-start | bytes 1156

commit v3 on v2

--- a/solution.py
+++ b/solution.py
@@ -20,6 +20,7 @@
 LANE_STEPS = 7
 STEPS = 13
 REACH = 32
+FAR = 56
 
 
 def tables(lat_count):
@@ -48,9 +49,9 @@
     n, side, cores, at,
     x_hbm, mask2d, speed2d, angle2d, tab,
     out, height_out, mean_out,
-    x, field_a, field_b, stage, shifts, go_left, go_right, hist,
+    x, field_a, field_b, stage, shifts, go_left, go_right, moved_a, moved_b,
     send, recv, back, home, flat, energy, rolled, own, low_part, high_part, heights,
-    send_sem, recv_sem, load_sem,
+    send_sem, recv_sem, load_sem, column_sem,
 ):
     bins_dev, cells = x.shape
     half = bins_dev // 2
@@ -87,9 +88,22 @@
             act(me - my_c + lax.rem(my_c + c, cores))
 
     barrier = pltpu.get_barrier_semaphore()
-    peers(
-        lambda to: pl.semaphore_signal(barrier, inc=1, device_id={"spec": to}, device_id_type=MESH)
-    )
+
+    def call_row(i, carry):
+        to = (lax.rem(my_x + i // cores, side) * side + my_y) * cores + lax.rem(my_c + lax.rem(i, cores), cores)
+        pl.semaphore_signal(barrier, inc=1, device_id={"spec": to}, device_id_type=MESH)
+        return carry
+
+    def call_column(semaphore):
+        def one(i, carry):
+            to = (my_x * side + lax.rem(my_y + i, side)) * cores + my_c
+            pl.semaphore_signal(semaphore, inc=1, device_id={"spec": to}, device_id_type=MESH)
+            return carry
+
+        lax.fori_loop(1, side, one, 0)
+
+    lax.fori_loop(1, side * cores, call_row, 0)
+    call_column(barrier)
 
     lane = lax.broadcasted_iota(jnp.int32, (8, 128), 1)
     row = lax.broadcasted_iota(jnp.int32, (8, 128), 0)
@@ -110,6 +124,7 @@
         jnp.ones((128, 128), jnp.bfloat16),
         preferred_element_type=jnp.float32,
     )
+    inner = slice(REACH, REACH + chunks)
     shifts[0:chunks, :] = jnp.where(is_sea, count.astype(jnp.int32), 0)
     shifts[chunks:, :] = jnp.zeros((shifts.shape[0] - chunks, 128), jnp.int32)
     go_left[...] = jnp.zeros_like(go_left)
@@ -119,8 +134,8 @@
     def settle(left, incoming, d):
         goes = jnp.bitwise_and(left, d)
         comes = jnp.bitwise_and(incoming, d)
-        go_right[...] += goes
-        go_left[...] += comes
+        go_right[inner, :] += goes
+        go_left[inner, :] += comes
         shifts[0:chunks, :] = jnp.where(comes != 0, incoming, jnp.where(goes != 0, 0, left))
 
     def lane_step(i, carry):
@@ -174,8 +189,8 @@
         src, dst = (field_a, field_b) if s % 2 == 0 else (field_b, field_a)
 
         def advance(g, carry, src=src, dst=dst, s=s):
-            for ru in range(2):
-                r = g * 2 + ru
+            for ru in range(4):
+                r = g * 4 + ru
                 widen = tab[pl.ds(at["widen"] + r, 1), :]
                 first = pad + r * per_row
                 for t in range(2):
@@ -200,18 +215,57 @@
                             dst[t, first + q] = jnp.where(row == half, wind, new)
             return carry
 
-        lax.fori_loop(0, lat_count // 2, advance, 0)
+        lax.fori_loop(0, lat_count // 4, advance, 0)
     final = field_a if SUBSTEPS % 2 == 0 else field_b
 
+    pl.semaphore_wait(barrier, side * cores + side - 2)
+    call_column(column_sem)
+
     unroll = 8
 
-    def gather(g, carry):
+    def word_of(words, v):
+        return jnp.broadcast_to(words[pl.ds(REACH + v, 1), :], (8, 128))
+
+    def has(word, i):
+        return jnp.bitwise_and(word, 1 << i) != 0
+
+    def near_rows(words, src, dst, toward_end, bit_order):
+        way = 1 if toward_end else -1
+
+        def block(g, carry):
+            first = g * unroll
+            span = [first + way * u if toward_end else first + unroll - 1 - u for u in range(unroll + 7)]
+            word = [word_of(words, v) for v in span]
+            for t in range(2):
+                cur = [src[t, FAR + v] for v in span]
+                for b in bit_order:
+                    d = 1 << b
+                    cur = [
+                        jnp.where(has(word[u], LANE_STEPS + b), cur[u + d], cur[u])
+                        for u in range(len(cur) - d)
+                    ]
+                for u in range(unroll):
+                    dst[t, FAR + span[u]] = cur[u]
+            return carry
+
+        lax.fori_loop(0, chunks // unroll, block, 0)
+
+    def far_rows(words, src, t, v, way, bit_order):
+        def value(v, order):
+            if not order:
+                return src[t, FAR + v]
+            d = way * (1 << order[-1])
+            return jnp.where(
+                has(word_of(words, v), LANE_STEPS + order[-1]), value(v + d, order[:-1]), value(v, order[:-1])
+            )
+
+        return value(v, bit_order)
+
+    def lanes_left(g, carry):
         turned = list(carry)
         for u in range(unroll):
             v = chunks - 1 - (g * unroll + u)
-            word = jnp.broadcast_to(go_left[pl.ds(v, 1), :], (8, 128))
-            moves = [jnp.bitwise_and(word, 1 << i) != 0 for i in range(STEPS)]
-            cur = []
+            word = word_of(go_left, v)
             for t in range(2):
                 a = final[t, pad + v]
                 for i in range(LANE_STEPS):
@@ -219,20 +273,24 @@
                     rot = pltpu.roll(a, 128 - d, 1)
                     b = jnp.where(lane < 128 - d, rot, turned[t * LANE_STEPS + i])
                     turned[t * LANE_STEPS + i] = rot
-                    a = jnp.where(moves[i], b, a)
-                for i in range(LANE_STEPS, STEPS):
-                    dv = 1 << (i - LANE_STEPS)
-                    hist[i - LANE_STEPS, t, v] = a
-                    a = jnp.where(moves[i], hist[i - LANE_STEPS, t, v + dv], a)
-                cur.append(a)
-            even, odd = cur
-            send[2 * v] = jnp.where(low, even, pltpu.roll(odd, 64, 1))
-            send[2 * v + 1] = jnp.where(low, pltpu.roll(even, 64, 1), odd)
+                    a = jnp.where(has(word, i), b, a)
+                moved_a[t, FAR + v] = a
         return tuple(turned)
 
-    lax.fori_loop(0, chunks // unroll, gather, (zero,) * (2 * LANE_STEPS))
-
-    pl.semaphore_wait(barrier, n - 1)
+    lax.fori_loop(0, chunks // unroll, lanes_left, (zero,) * (2 * LANE_STEPS))
+    near_rows(go_left, moved_a, moved_b, True, (0, 1, 2))
+
+    def pack(g, carry):
+        for u in range(4):
+            v = g * 4 + u
+            even, odd = (far_rows(go_left, moved_b, t, v, 1, (3, 4, 5)) for t in range(2))
+            send[2 * v] = jnp.where(low, even, pltpu.roll(odd, SEA_DEV, 1))
+            send[2 * v + 1] = jnp.where(low, pltpu.roll(even, SEA_DEV, 1), odd)
+        return carry
+
+    lax.fori_loop(0, n * SEA_DEV // 128 // 4, pack, 0)
+
+    pl.semaphore_wait(column_sem, side - 1)
 
     def exchange(src, dst, rows, k):
         def push(to):
@@ -355,30 +413,40 @@
     finish(send, half, send_sem.at[0])
     finish(home, half + 1, recv_sem.at[1])
 
-    def scatter(g, carry):
+    def unpack(g, carry):
+        for u in range(unroll):
+            v = g * unroll + u
+            a, b = home[2 * v], home[2 * v + 1]
+            moved_a[0, FAR + v] = jnp.where(low, a, pltpu.roll(b, SEA_DEV, 1))
+            moved_a[1, FAR + v] = jnp.where(low, pltpu.roll(a, SEA_DEV, 1), b)
+        return carry
+
+    lax.fori_loop(0, n * SEA_DEV // 128 // unroll, unpack, 0)
+
+    def spread(g, carry):
+        for u in range(4):
+            v = g * 4 + u
+            for t in range(2):
+                moved_b[t, FAR + v] = far_rows(go_right, moved_a, t, v, -1, (5, 4, 3))
+        return carry
+
+    lax.fori_loop(0, chunks // 4, spread, 0)
+    near_rows(go_right, moved_b, moved_a, False, (2, 1, 0))
+
+    def lanes_right(g, carry):
         turned = list(carry)
         for u in range(unroll):
             v = g * unroll + u
-            word = jnp.broadcast_to(go_right[pl.ds(v, 1), :], (8, 128))
-            moves = [jnp.bitwise_and(word, 1 << i) != 0 for i in range(STEPS)]
-            sea = jnp.broadcast_to(mask2d[pl.ds(v, 1), :], (8, 128)) != 0
-            a, b = home[2 * v], home[2 * v + 1]
-            cur = [
-                jnp.where(low, a, pltpu.roll(b, SEA_DEV, 1)),
-                jnp.where(low, pltpu.roll(a, SEA_DEV, 1), b),
-            ]
+            word = word_of(go_right, v)
+            sea = jnp.broadcast_to(sea_row(v), (8, 128))
             for t in range(2):
-                a = cur[t]
-                for i in range(STEPS - 1, LANE_STEPS - 1, -1):
-                    dv = 1 << (i - LANE_STEPS)
-                    hist[i - LANE_STEPS, t, REACH + v] = a
-                    a = jnp.where(moves[i], hist[i - LANE_STEPS, t, REACH + v - dv], a)
+                a = moved_a[t, FAR + v]
                 for i in range(LANE_STEPS - 1, -1, -1):
                     d = 1 << i
                     rot = pltpu.roll(a, d, 1)
                     b = jnp.where(lane < d, turned[t * LANE_STEPS + i], rot)
                     turned[t * LANE_STEPS + i] = rot
-                    a = jnp.where(moves[i], b, a)
+                    a = jnp.where(has(word, i), b, a)
                 a = jnp.where(sea, a, 0.0)
                 stage[u, pl.ds(t, half, stride=2), :] = a[0:half]
                 if t == 0:
@@ -386,7 +454,7 @@
             out[:, pl.ds(pl.multiple_of(v * 128, 128), 128)] = stage[u, 0:bins_dev, :]
         return tuple(turned)
 
-    lax.fori_loop(0, chunks // unroll, scatter, (zero,) * (2 * LANE_STEPS))
+    lax.fori_loop(0, chunks // unroll, lanes_right, (zero,) * (2 * LANE_STEPS))
 
     points = cells // n
     together = NLON // points
@@ -422,7 +490,7 @@
         padded = chunks + 2 * (NLON // 128)
         tab, at = tables(cells // NLON)
         vmem = pl.BlockSpec(memory_space=pltpu.VMEM)
-        words = pltpu.VMEM((chunks, 128), jnp.int32)
+        words = pltpu.VMEM((chunks + 2 * REACH, 128), jnp.int32)
         by_freq = lambda *dims: pltpu.VMEM((*dims, PAIRS, 128), jnp.float32)
         messages = lambda count: pltpu.VMEM((count, 8, 128), jnp.float32)
         new_spectrum, height, mean = pl.pallas_call(
@@ -443,11 +511,12 @@
                 pltpu.VMEM((chunks + REACH, 128), jnp.int32),
                 words,
                 words,
-                pltpu.VMEM((STEPS - LANE_STEPS, 2, chunks + REACH, 8, 128), jnp.float32),
-                messages(2 * chunks),
+                pltpu.VMEM((2, chunks + 2 * FAR, 8, 128), jnp.float32),
+                pltpu.VMEM((2, chunks + 2 * FAR, 8, 128), jnp.float32),
                 messages(n),
                 messages(n),
-                messages(2 * chunks),
+                messages(n),
+                messages(n),
                 pltpu.VMEM((n // 8, 8 * bins_dev // 2, 128), jnp.float32),
                 by_freq(NF),
                 by_freq(4, NF + 5),
@@ -458,6 +527,7 @@
                 pltpu.SemaphoreType.DMA((2,)),
                 pltpu.SemaphoreType.DMA((2,)),
                 pltpu.SemaphoreType.DMA,
+                pltpu.SemaphoreType.REGULAR,
             ],
             compiler_params=pltpu.CompilerParams(collective_id=0, has_side_effects=True),
         )(

time: 84.5 us -> 74.7 us (0.88)
  Pallas kernels: 79.3 us -> 69.6 us
    pallas_call x1, Pallas kernels: 79.3 us -> 69.6 us  [local(): pl.pallas_call(functools.partial(step_kernel, n, side, cores, at), name='...]
where the time goes in v3:
time: 74.7 us; the launch traced here: 74.5 us
  Pallas kernels  69.6 us (93%)
  local copies, waits for them, and re-layouts  2.58 us (3%)
  between operations  2.4 us (3%)
    pallas_call x1, Pallas kernels, local(): pl.pallas_call(functools.partial(step_kernel, n, side, cores, at), name='...  69.6 us
    unnamed x4, local copies, waits for them, and re-layouts  2.58 us

profile of v3, /device:TPU:513, one launch (start us, length us, event | category | flops | bytes accessed | tf_op | source)
XLA Modules:
  0.0 74.5 jit_solution(5413994034550947523)
XLA Ops:
  0.6 69.6 %wave_step.1 = (f32[12,12288]{1,0:T(8,128)}, f32[1,96]{1,0:T(1,128)}, f32[1,1]{1,0:T(1,128)}) custom-call(f32[12,12288]{1,0:T(8,128)} %x_hbm.1, s32[96,128]{1,0:T(8,128)} %bitcast.5, f32[96,128]{1,0:T(8,128)} %bitcast.6, f32[96,128]{1,0:T(8,128)} %bitcast.7, f32[272,128]{1,0:T(8,128)} %constant.2.clone.tab), custom_call_target="tpu_custom_call" | custom-call | tf_op jit(solution)/shard_map/wave_step/pallas_call | solution.py:496
  70.2 0.0 copy-start
  70.2 2.1 %copy.11 = f32[12,12288]{1,0:T(8,128)} copy(f32[12,12288]{1,0:T(8,128)} %get-tuple-element.12) | data formatting | bytes 1179648
  72.3 0.0 copy-done
  72.3 0.5 copy.12
Async XLA Ops:
  70.2 2.1 %copy-start = (f32[1,96]{1,0:T(1,128)S(1)}, f32[1,96]{1,0:T(1,128)}, u32[]{:S(2)}) copy-start(f32[1,96]{1,0:T(1,128)} %get-tuple-element.7) | copy-start | bytes 1156

commit v4 on v3

--- a/solution.py
+++ b/solution.py
@@ -17,8 +17,7 @@
 MESH = pl.DeviceIdType.MESH
 LOG_RATIO = math.log(1.1)
 PAIRS = ND // 2
-LANE_STEPS = 7
-STEPS = 13
+ROW_STEPS = 6
 REACH = 32
 FAR = 56
 
@@ -49,7 +48,7 @@
     n, side, cores, at,
     x_hbm, mask2d, speed2d, angle2d, tab,
     out, height_out, mean_out,
-    x, field_a, field_b, stage, shifts, go_left, go_right, moved_a, moved_b,
+    x, field_a, field_b, stage, shifts, go_left, go_right, pick, put, moved_a, moved_b,
     send, recv, back, home, flat, energy, rolled, own, low_part, high_part, heights,
     send_sem, recv_sem, load_sem, column_sem,
 ):
@@ -111,45 +110,45 @@
 
     is_sea = mask2d[...] != 0
     land = jnp.where(is_sea, 0.0, 1.0).astype(jnp.bfloat16)
-    before = (
+    earlier = (
         lax.broadcasted_iota(jnp.int32, (128, 128), 0) < lax.broadcasted_iota(jnp.int32, (128, 128), 1)
     ).astype(jnp.bfloat16)
     above = (
         lax.broadcasted_iota(jnp.int32, (chunks, chunks), 1)
         < lax.broadcasted_iota(jnp.int32, (chunks, chunks), 0)
     ).astype(jnp.bfloat16)
-    rows_above = jnp.dot(above, land, preferred_element_type=jnp.float32)
-    count = jnp.dot(land, before, preferred_element_type=jnp.float32) + jnp.dot(
-        rows_above.astype(jnp.bfloat16),
-        jnp.ones((128, 128), jnp.bfloat16),
-        preferred_element_type=jnp.float32,
-    )
-    inner = slice(REACH, REACH + chunks)
-    shifts[0:chunks, :] = jnp.where(is_sea, count.astype(jnp.int32), 0)
+    ones = jnp.ones((128, 128), jnp.bfloat16)
+    count = functools.partial(jnp.dot, preferred_element_type=jnp.float32)
+    before = count(land, earlier).astype(jnp.int32)
+    sea_in_row = 128 - count(land, ones).astype(jnp.int32)
+    wide_lane = lax.broadcasted_iota(jnp.int32, (chunks, 128), 1)
+    wide_row = lax.broadcasted_iota(jnp.int32, (chunks, 128), 0)
+    rank0 = wide_row * 128 - count(count(above, land).astype(jnp.bfloat16), ones).astype(jnp.int32)
+    put[...] = jnp.bitwise_and(rank0 + wide_lane - before, 127)
+    to_go = jnp.where(is_sea, before, 0)
     shifts[chunks:, :] = jnp.zeros((shifts.shape[0] - chunks, 128), jnp.int32)
     go_left[...] = jnp.zeros_like(go_left)
     go_right[...] = jnp.zeros_like(go_right)
-    wide_lane = lax.broadcasted_iota(jnp.int32, (chunks, 128), 1)
-
-    def settle(left, incoming, d):
-        goes = jnp.bitwise_and(left, d)
-        comes = jnp.bitwise_and(incoming, d)
-        go_right[inner, :] += goes
-        go_left[inner, :] += comes
-        shifts[0:chunks, :] = jnp.where(comes != 0, incoming, jnp.where(goes != 0, 0, left))
-
-    def lane_step(i, carry):
+
+    def close_up(i, to_go):
         d = jnp.left_shift(1, i)
-        left = shifts[0:chunks, :]
-        near = pltpu.roll(left, 128 - d, 1)
-        far = pltpu.roll(shifts[1 : chunks + 1, :], 128 - d, 1)
-        settle(left, jnp.where(wide_lane < 128 - d, near, far), d)
-        return carry
-
-    lax.fori_loop(0, LANE_STEPS, lane_step, 0)
-    for i in range(LANE_STEPS, STEPS):
-        dv = 1 << (i - LANE_STEPS)
-        settle(shifts[0:chunks, :], shifts[dv : chunks + dv, :], 1 << i)
+        incoming = pltpu.roll(to_go, 128 - d, 1)
+        stay = jnp.where(jnp.bitwise_and(to_go, d) != 0, 0, to_go)
+        return jnp.where(jnp.bitwise_and(incoming, d) != 0, incoming, stay)
+
+    def plan_rows(to_go):
+        nth = jnp.bitwise_and(wide_lane - rank0, 127)
+        front = jnp.bitwise_and(wide_lane + to_go, 127)
+        pick[...] = jnp.take_along_axis(front, nth, axis=1, mode="promise_in_bounds")
+        up = wide_row - jnp.right_shift(rank0 + nth, 7)
+        shifts[0:chunks, :] = jnp.where(nth < sea_in_row, up, 0)
+        for b in range(ROW_STEPS):
+            here, incoming = shifts[0:chunks, :], shifts[1 << b : chunks + (1 << b), :]
+            goes = jnp.bitwise_and(here, 1 << b)
+            comes = jnp.bitwise_and(incoming, 1 << b)
+            go_right[REACH : REACH + chunks, :] += goes
+            go_left[REACH : REACH + chunks, :] += comes
+            shifts[0:chunks, :] = jnp.where(comes != 0, incoming, jnp.where(goes != 0, 0, here))
 
     zero = jnp.zeros((8, 128), jnp.float32)
     pad = per_row
@@ -185,10 +184,16 @@
 
     lax.fori_loop(0, chunks // 8, split_bins, 0)
 
+    def lanes(tile, index, v):
+        index = jnp.broadcast_to(index[pl.ds(v, 1), :], (8, 128))
+        return jnp.take_along_axis(tile, index, axis=1, mode="promise_in_bounds")
+
     for s in range(SUBSTEPS):
         src, dst = (field_a, field_b) if s % 2 == 0 else (field_b, field_a)
 
-        def advance(g, carry, src=src, dst=dst, s=s):
+        def advance(g, to_go, src=src, dst=dst, s=s):
+            if s == 0:
+                to_go = close_up(g, to_go)
             for ru in range(4):
                 r = g * 4 + ru
                 widen = tab[pl.ds(at["widen"] + r, 1), :]
@@ -212,11 +217,13 @@
                             dst[t, first + q] = jnp.where(sea_row(v), new, 0.0)
                         else:
                             wind = (speed2d, angle2d)[t][pl.ds(v, 1), :]
-                            dst[t, first + q] = jnp.where(row == half, wind, new)
-            return carry
-
-        lax.fori_loop(0, lat_count // 4, advance, 0)
-    final = field_a if SUBSTEPS % 2 == 0 else field_b
+                            new = jnp.where(row == half, wind, new)
+                            moved_a[t, FAR + v] = lanes(new, pick, v)
+            return to_go
+
+        to_go = lax.fori_loop(0, lat_count // 4, advance, to_go)
+        if s == 0:
+            plan_rows(to_go)
 
     pl.semaphore_wait(barrier, side * cores + side - 2)
     call_column(column_sem)
@@ -229,7 +236,7 @@
     def has(word, i):
         return jnp.bitwise_and(word, 1 << i) != 0
 
-    def near_rows(words, src, dst, toward_end, bit_order):
+    def near_rows(words, src, emit, toward_end, bit_order):
         way = 1 if toward_end else -1
 
         def block(g, carry):
@@ -241,11 +248,11 @@
                 for b in bit_order:
                     d = 1 << b
                     cur = [
-                        jnp.where(has(word[u], LANE_STEPS + b), cur[u + d], cur[u])
+                        jnp.where(has(word[u], b), cur[u + d], cur[u])
                         for u in range(len(cur) - d)
                     ]
                 for u in range(unroll):
-                    dst[t, FAR + span[u]] = cur[u]
+                    emit(t, u, span[u], cur[u])
             return carry
 
         lax.fori_loop(0, chunks // unroll, block, 0)
@@ -256,39 +263,25 @@
                 return src[t, FAR + v]
             d = way * (1 << order[-1])
             return jnp.where(
-                has(word_of(words, v), LANE_STEPS + order[-1]), value(v + d, order[:-1]), value(v, order[:-1])
+                has(word_of(words, v), order[-1]), value(v + d, order[:-1]), value(v, order[:-1])
             )
 
         return value(v, bit_order)
 
-    def lanes_left(g, carry):
-        turned = list(carry)
+    def keep_near(t, u, v, tile):
+        moved_b[t, FAR + v] = tile
+
+    near_rows(go_left, moved_a, keep_near, True, (0, 1, 2))
+
+    def pack(g, carry):
         for u in range(unroll):
-            v = chunks - 1 - (g * unroll + u)
-            word = word_of(go_left, v)
-            for t in range(2):
-                a = final[t, pad + v]
-                for i in range(LANE_STEPS):
-                    d = 1 << i
-                    rot = pltpu.roll(a, 128 - d, 1)
-                    b = jnp.where(lane < 128 - d, rot, turned[t * LANE_STEPS + i])
-                    turned[t * LANE_STEPS + i] = rot
-                    a = jnp.where(has(word, i), b, a)
-                moved_a[t, FAR + v] = a
-        return tuple(turned)
-
-    lax.fori_loop(0, chunks // unroll, lanes_left, (zero,) * (2 * LANE_STEPS))
-    near_rows(go_left, moved_a, moved_b, True, (0, 1, 2))
-
-    def pack(g, carry):
-        for u in range(4):
-            v = g * 4 + u
+            v = g * unroll + u
             even, odd = (far_rows(go_left, moved_b, t, v, 1, (3, 4, 5)) for t in range(2))
             send[2 * v] = jnp.where(low, even, pltpu.roll(odd, SEA_DEV, 1))
             send[2 * v + 1] = jnp.where(low, pltpu.roll(even, SEA_DEV, 1), odd)
         return carry
 
-    lax.fori_loop(0, n * SEA_DEV // 128 // 4, pack, 0)
+    lax.fori_loop(0, n * SEA_DEV // 128 // unroll, pack, 0)
 
     pl.semaphore_wait(column_sem, side - 1)
 
@@ -344,21 +337,23 @@
     per_group = half * group // PAIRS
     finish(recv, half, recv_sem.at[0])
 
-    def arrange(g, carry):
+    def arrange(h, carry):
         m0, m1 = carry
-        for i in range(group):
-            flat[g, half * i : half * i + half, :] = recv[g * group + i, 0:half, :]
-        for q in range(per_group):
-            k = g * per_group + q
-            a = flat[g, PAIRS * q : PAIRS * (q + 1), :]
-            energy[k] = a
-            m0 = m0 + a
-            m1 = m1 + tab[pl.ds(at["omega"] + k, 1), :] * a
-            for w, b in enumerate(turns(a, (1, -1, 3, -3))):
-                rolled[w, k + 3] = b
+        for g in (2 * h, 2 * h + 1):
+            for i in range(group):
+                flat[g, half * i : half * i + half, :] = recv[g * group + i, 0:half, :]
+        for g in (2 * h, 2 * h + 1):
+            for q in range(per_group):
+                k = g * per_group + q
+                a = flat[g, PAIRS * q : PAIRS * (q + 1), :]
+                energy[k] = a
+                m0 = m0 + a
+                m1 = m1 + tab[pl.ds(at["omega"] + k, 1), :] * a
+                for w, b in enumerate(turns(a, (1, -1, 3, -3))):
+                    rolled[w, k + 3] = b
         return m0, m1
 
-    m0, m1 = lax.fori_loop(0, n // group, arrange, (zero16, zero16))
+    m0, m1 = lax.fori_loop(0, n // group // 2, arrange, (zero16, zero16))
 
     def over_bins(a):
         a = jnp.sum(a, axis=0, keepdims=True)
@@ -370,8 +365,8 @@
     breaking = steep * steep / (1.0 + steep * steep)
 
     def transfer(g, carry):
-        for q in range(per_group):
-            k = g * per_group + q
+        for q in range(2 * per_group):
+            k = g * 2 * per_group + q
             a = energy[k]
             factor = tab[pl.ds(at["rate"] + k, 1), :] * a
             rates = []
@@ -383,7 +378,7 @@
             high_part[k] = up[1] + down[1]
         return carry
 
-    lax.fori_loop(0, n // group, transfer, 0)
+    lax.fori_loop(0, n // group // 2, transfer, 0)
 
     def renew(g, total):
         for q in range(per_group):
@@ -414,14 +409,14 @@
     finish(home, half + 1, recv_sem.at[1])
 
     def unpack(g, carry):
-        for u in range(unroll):
-            v = g * unroll + u
+        for u in range(2 * unroll):
+            v = g * 2 * unroll + u
             a, b = home[2 * v], home[2 * v + 1]
             moved_a[0, FAR + v] = jnp.where(low, a, pltpu.roll(b, SEA_DEV, 1))
             moved_a[1, FAR + v] = jnp.where(low, pltpu.roll(a, SEA_DEV, 1), b)
         return carry
 
-    lax.fori_loop(0, n * SEA_DEV // 128 // unroll, unpack, 0)
+    lax.fori_loop(0, n * SEA_DEV // 128 // (2 * unroll), unpack, 0)
 
     def spread(g, carry):
         for u in range(4):
@@ -431,30 +426,16 @@
         return carry
 
     lax.fori_loop(0, chunks // 4, spread, 0)
-    near_rows(go_right, moved_b, moved_a, False, (2, 1, 0))
-
-    def lanes_right(g, carry):
-        turned = list(carry)
-        for u in range(unroll):
-            v = g * unroll + u
-            word = word_of(go_right, v)
-            sea = jnp.broadcast_to(sea_row(v), (8, 128))
-            for t in range(2):
-                a = moved_a[t, FAR + v]
-                for i in range(LANE_STEPS - 1, -1, -1):
-                    d = 1 << i
-                    rot = pltpu.roll(a, d, 1)
-                    b = jnp.where(lane < d, turned[t * LANE_STEPS + i], rot)
-                    turned[t * LANE_STEPS + i] = rot
-                    a = jnp.where(has(word, i), b, a)
-                a = jnp.where(sea, a, 0.0)
-                stage[u, pl.ds(t, half, stride=2), :] = a[0:half]
-                if t == 0:
-                    heights[pl.ds(v, 1), :] = a[half : half + 1]
+
+    def deliver(t, u, v, tile):
+        tile = jnp.where(jnp.broadcast_to(sea_row(v), (8, 128)), lanes(tile, put, v), 0.0)
+        stage[u, pl.ds(t, half, stride=2), :] = tile[0:half]
+        if t == 0:
+            heights[pl.ds(v, 1), :] = tile[half : half + 1]
+        else:
             out[:, pl.ds(pl.multiple_of(v * 128, 128), 128)] = stage[u, 0:bins_dev, :]
-        return tuple(turned)
-
-    lax.fori_loop(0, chunks // unroll, lanes_right, (zero,) * (2 * LANE_STEPS))
+
+    near_rows(go_right, moved_b, deliver, False, (2, 1, 0))
 
     points = cells // n
     together = NLON // points
@@ -511,6 +492,8 @@
                 pltpu.VMEM((chunks + REACH, 128), jnp.int32),
                 words,
                 words,
+                pltpu.VMEM((chunks, 128), jnp.int32),
+                pltpu.VMEM((chunks, 128), jnp.int32),
                 pltpu.VMEM((2, chunks + 2 * FAR, 8, 128), jnp.float32),
                 pltpu.VMEM((2, chunks + 2 * FAR, 8, 128), jnp.float32),
                 messages(n),

time: 74.7 us -> 63.9 us (0.86)
  Pallas kernels: 69.6 us -> 58.7 us
    pallas_call x1, Pallas kernels: 69.6 us -> 58.7 us  [local(): pl.pallas_call(functools.partial(step_kernel, n, side, cores, at), name='...]
where the time goes in v4:
time: 63.9 us; the launch traced here: 63.7 us
  Pallas kernels  58.7 us (92%)
  local copies, waits for them, and re-layouts  2.58 us (4%)
  between operations  2.4 us (4%)
    pallas_call x1, Pallas kernels, local(): pl.pallas_call(functools.partial(step_kernel, n, side, cores, at), name='...  58.7 us
    unnamed x4, local copies, waits for them, and re-layouts  2.58 us

profile of v4, /device:TPU:513, one launch (start us, length us, event | category | flops | bytes accessed | tf_op | source)
XLA Modules:
  0.0 63.7 jit_solution(1232550812203218571)
XLA Ops:
  0.6 58.7 %wave_step.1 = (f32[12,12288]{1,0:T(8,128)}, f32[1,96]{1,0:T(1,128)}, f32[1,1]{1,0:T(1,128)}) custom-call(f32[12,12288]{1,0:T(8,128)} %x_hbm.1, s32[96,128]{1,0:T(8,128)} %bitcast.5, f32[96,128]{1,0:T(8,128)} %bitcast.6, f32[96,128]{1,0:T(8,128)} %bitcast.7, f32[272,128]{1,0:T(8,128)} %constant.2.clone.tab), custom_call_target="tpu_custom_call" | custom-call | tf_op jit(solution)/shard_map/wave_step/pallas_call | solution.py:477
  59.3 0.0 copy-start
  59.3 2.1 %copy.11 = f32[12,12288]{1,0:T(8,128)} copy(f32[12,12288]{1,0:T(8,128)} %get-tuple-element.12) | data formatting | bytes 1179648
  61.4 0.0 copy-done
  61.4 0.5 copy.12
Async XLA Ops:
  59.3 2.1 %copy-start = (f32[1,96]{1,0:T(1,128)S(1)}, f32[1,96]{1,0:T(1,128)}, u32[]{:S(2)}) copy-start(f32[1,96]{1,0:T(1,128)} %get-tuple-element.7) | copy-start | bytes 1156

commit v5 on v4

--- a/solution.py
+++ b/solution.py
@@ -46,9 +46,9 @@
 
 def step_kernel(
     n, side, cores, at,
-    x_hbm, mask2d, speed2d, angle2d, tab,
+    x_hbm, mask_hbm, speed_hbm, angle_hbm, tab_hbm,
     out, height_out, mean_out,
-    x, field_a, field_b, stage, shifts, go_left, go_right, pick, put, moved_a, moved_b,
+    x, mask2d, speed2d, angle2d, tab, field_a, field_b, stage, shifts, go_left, go_right, pick, put, moved_a, moved_b,
     send, recv, back, home, flat, energy, rolled, own, low_part, high_part, heights,
     send_sem, recv_sem, load_sem, column_sem,
 ):
@@ -60,31 +60,66 @@
     me = lax.axis_index("spec")
     my_x, my_y, my_c = me // (side * cores), lax.rem(me // cores, side), lax.rem(me, cores)
 
-    load = pltpu.make_async_copy(x_hbm, x, load_sem)
-    load.start()
+    parts = 4
+    part_cols = cells // parts
+    small = [
+        pltpu.make_async_copy(src, dst, load_sem.at[parts + k])
+        for k, (src, dst) in enumerate(
+            ((mask_hbm, mask2d), (tab_hbm, tab), (speed_hbm, speed2d), (angle_hbm, angle2d))
+        )
+    ]
+
+    def load(part):
+        cols = pl.ds(pl.multiple_of(part * part_cols, 128), part_cols)
+        return pltpu.make_async_copy(x_hbm.at[:, cols], x.at[:, cols], load_sem.at[part])
+
+    small[0].start()
+    for part in range(parts):
+        load(part).start()
+    for copy in small[1:]:
+        copy.start()
+
+    def hop(u):
+        return side // 2 + jnp.where(lax.rem(u, 2) == 0, u // 2, -((u + 1) // 2))
+
+    def both_cores(act, px, py):
+        first = (px * side + py) * cores
+        act(first + my_c)
+        for c in range(1, cores):
+            act(first + lax.rem(my_c + c, cores))
+
+    def own_chip(act):
+        for c in range(1, cores):
+            act(me - my_c + lax.rem(my_c + c, cores))
 
     def peers(act):
-        def hop(u):
-            return side // 2 + jnp.where(lax.rem(u, 2) == 0, u // 2, -((u + 1) // 2))
-
-        def chip(s, u):
-            px = lax.rem(my_x + hop(u), side)
-            py = lax.rem(my_y + hop(s - u), side)
-            first = (px * side + py) * cores
-            act(first + my_c)
-            for c in range(1, cores):
-                act(first + lax.rem(my_c + c, cores))
-
         def diagonal(s, carry):
             def one(u, inner):
-                chip(s, u)
+                both_cores(act, lax.rem(my_x + hop(u), side), lax.rem(my_y + hop(s - u), side))
                 return inner
 
             return lax.fori_loop(jnp.maximum(0, s - side + 1), jnp.minimum(side - 1, s) + 1, one, carry)
 
         lax.fori_loop(0, 2 * side - 2, diagonal, 0)
-        for c in range(1, cores):
-            act(me - my_c + lax.rem(my_c + c, cores))
+        own_chip(act)
+
+    def peers_by_row(act):
+        def row_of(py, count):
+            def one(u, inner):
+                both_cores(act, lax.rem(my_x + hop(u), side), py)
+                return inner
+
+            lax.fori_loop(0, count, one, 0)
+
+        def far_row(i, carry):
+            py = lax.rem(my_y + hop(i), side)
+            pl.semaphore_wait(column_sem.at[py], 1)
+            row_of(py, side)
+            return carry
+
+        lax.fori_loop(0, side - 1, far_row, 0)
+        row_of(my_y, side - 1)
+        own_chip(act)
 
     barrier = pltpu.get_barrier_semaphore()
 
@@ -103,6 +138,7 @@
 
     lax.fori_loop(1, side * cores, call_row, 0)
     call_column(barrier)
+    small[0].wait()
 
     lane = lax.broadcasted_iota(jnp.int32, (8, 128), 1)
     row = lax.broadcasted_iota(jnp.int32, (8, 128), 0)
@@ -124,7 +160,8 @@
     wide_lane = lax.broadcasted_iota(jnp.int32, (chunks, 128), 1)
     wide_row = lax.broadcasted_iota(jnp.int32, (chunks, 128), 0)
     rank0 = wide_row * 128 - count(count(above, land).astype(jnp.bfloat16), ones).astype(jnp.int32)
-    put[...] = jnp.bitwise_and(rank0 + wide_lane - before, 127)
+    put[0] = jnp.bitwise_and(rank0 + wide_lane - before, 127)
+    put[1] = jnp.bitwise_and(rank0 + wide_lane - before + SEA_DEV, 127)
     to_go = jnp.where(is_sea, before, 0)
     shifts[chunks:, :] = jnp.zeros((shifts.shape[0] - chunks, 128), jnp.int32)
     go_left[...] = jnp.zeros_like(go_left)
@@ -139,16 +176,20 @@
     def plan_rows(to_go):
         nth = jnp.bitwise_and(wide_lane - rank0, 127)
         front = jnp.bitwise_and(wide_lane + to_go, 127)
-        pick[...] = jnp.take_along_axis(front, nth, axis=1, mode="promise_in_bounds")
+        took = jnp.take_along_axis(front, nth, axis=1, mode="promise_in_bounds")
+        pick[0] = took
+        pick[1] = pltpu.roll(took, SEA_DEV, 1)
         up = wide_row - jnp.right_shift(rank0 + nth, 7)
         shifts[0:chunks, :] = jnp.where(nth < sea_in_row, up, 0)
         for b in range(ROW_STEPS):
             here, incoming = shifts[0:chunks, :], shifts[1 << b : chunks + (1 << b), :]
             goes = jnp.bitwise_and(here, 1 << b)
             comes = jnp.bitwise_and(incoming, 1 << b)
-            go_right[REACH : REACH + chunks, :] += goes
-            go_left[REACH : REACH + chunks, :] += comes
+            rights, lefts = (goes, comes) if b == 0 else (rights + goes, lefts + comes)
             shifts[0:chunks, :] = jnp.where(comes != 0, incoming, jnp.where(goes != 0, 0, here))
+        for words, found in ((go_right, rights), (go_left, lefts)):
+            words[0, REACH : REACH + chunks, :] = found
+            words[1, REACH : REACH + chunks, :] = pltpu.roll(found, SEA_DEV, 1)
 
     zero = jnp.zeros((8, 128), jnp.float32)
     pad = per_row
@@ -158,6 +199,8 @@
                 f[t, v] = zero
                 f[t, pad + chunks + v] = zero
     base = (me * bins_dev) % ND
+    for copy in small[1:]:
+        copy.wait()
     cw, ce, cs, cn = [], [], [], []
     for t in range(2):
         k = ((me * bins_dev + jnp.minimum(2 * row + t, bins_dev - 1)) // ND).astype(jnp.float32)
@@ -168,7 +211,6 @@
         ce.append(-jnp.minimum(ax, 0.0))
         cs.append(jnp.maximum(ay, 0.0))
         cn.append(-jnp.minimum(ay, 0.0))
-    load.wait()
 
     def sea_row(v):
         return mask2d[pl.ds(v, 1), :] != 0
@@ -182,7 +224,12 @@
                 field_a[t, pad + v, 0:half, :] = stage[u, pl.ds(t, half, stride=2), :]
         return carry
 
-    lax.fori_loop(0, chunks // 8, split_bins, 0)
+    def split_part(part, carry):
+        load(part).wait()
+        per_part = chunks // 8 // parts
+        return lax.fori_loop(part * per_part, (part + 1) * per_part, split_bins, carry)
+
+    lax.fori_loop(0, parts, split_part, 0)
 
     def lanes(tile, index, v):
         index = jnp.broadcast_to(index[pl.ds(v, 1), :], (8, 128))
@@ -194,8 +241,14 @@
         def advance(g, to_go, src=src, dst=dst, s=s):
             if s == 0:
                 to_go = close_up(g, to_go)
+            else:
+                behind = jnp.maximum(g - 1, 0) * 4 * per_row
+                for u in range(4 * per_row):
+                    for t in range(2):
+                        v = behind + u
+                        moved_a[t, FAR + v] = lanes(dst[t, pad + v], pick.at[t], v)
             for ru in range(4):
-                r = g * 4 + ru
+                r = jnp.minimum(g, lat_count // 4 - 1) * 4 + ru
                 widen = tab[pl.ds(at["widen"] + r, 1), :]
                 first = pad + r * per_row
                 for t in range(2):
@@ -217,16 +270,15 @@
                             dst[t, first + q] = jnp.where(sea_row(v), new, 0.0)
                         else:
                             wind = (speed2d, angle2d)[t][pl.ds(v, 1), :]
-                            new = jnp.where(row == half, wind, new)
-                            moved_a[t, FAR + v] = lanes(new, pick, v)
+                            dst[t, first + q] = jnp.where(row == half, wind, new)
             return to_go
 
-        to_go = lax.fori_loop(0, lat_count // 4, advance, to_go)
+        to_go = lax.fori_loop(0, lat_count // 4 + min(s, 1), advance, to_go)
         if s == 0:
             plan_rows(to_go)
 
     pl.semaphore_wait(barrier, side * cores + side - 2)
-    call_column(column_sem)
+    call_column(column_sem.at[my_y])
 
     unroll = 8
 
@@ -242,8 +294,8 @@
         def block(g, carry):
             first = g * unroll
             span = [first + way * u if toward_end else first + unroll - 1 - u for u in range(unroll + 7)]
-            word = [word_of(words, v) for v in span]
             for t in range(2):
+                word = [word_of(words.at[t], v) for v in span]
                 cur = [src[t, FAR + v] for v in span]
                 for b in bit_order:
                     d = 1 << b
@@ -263,7 +315,7 @@
                 return src[t, FAR + v]
             d = way * (1 << order[-1])
             return jnp.where(
-                has(word_of(words, v), order[-1]), value(v + d, order[:-1]), value(v, order[:-1])
+                has(word_of(words.at[t], v), order[-1]), value(v + d, order[:-1]), value(v, order[:-1])
             )
 
         return value(v, bit_order)
@@ -277,43 +329,46 @@
         for u in range(unroll):
             v = g * unroll + u
             even, odd = (far_rows(go_left, moved_b, t, v, 1, (3, 4, 5)) for t in range(2))
-            send[2 * v] = jnp.where(low, even, pltpu.roll(odd, SEA_DEV, 1))
-            send[2 * v + 1] = jnp.where(low, pltpu.roll(even, SEA_DEV, 1), odd)
+            send[2 * v] = jnp.where(low, even, odd)
+            send[2 * v + 1] = jnp.where(low, odd, even)
         return carry
 
     lax.fori_loop(0, n * SEA_DEV // 128 // unroll, pack, 0)
 
-    pl.semaphore_wait(column_sem, side - 1)
-
-    def exchange(src, dst, rows, k):
+
+    def exchange(visit, src, dst, rows, k, arrival):
         def push(to):
             pltpu.make_async_remote_copy(
                 src_ref=src.at[to, pl.ds(0, rows)],
                 dst_ref=dst.at[me, pl.ds(0, rows)],
                 send_sem=send_sem.at[k],
-                recv_sem=recv_sem.at[k],
+                recv_sem=arrival,
                 device_id={"spec": to},
                 device_id_type=MESH,
             ).start()
 
-        peers(push)
-        dst[me] = src[me]
-
-    def finish(ref, rows, sem):
-        part = ref.at[pl.ds(0, n - 1), pl.ds(0, rows)]
+        visit(push)
+        pltpu.make_async_copy(src.at[me, pl.ds(0, rows)], dst.at[me, pl.ds(0, rows)], arrival).start()
+
+    def finish(ref, count, rows, sem):
+        part = ref.at[pl.ds(0, count), pl.ds(0, rows)]
         pltpu.make_async_copy(part, part, sem).wait()
 
-    exchange(send, recv, half, 0)
+    exchange(peers_by_row, send, recv, half, 0, recv_sem.at[my_x])
 
     wind = send[me][half : half + 1, :]
     other = pltpu.roll(wind, SEA_DEV, 1)
-    speed = jnp.where(low[0:1], wind, other)
-    angle = jnp.where(low[0:1], other, wind)
-    toward = speed * (
-        tab[at["pair_cos"] : at["pair_cos"] + PAIRS, :] * jnp.cos(angle)
-        + tab[at["pair_sin"] : at["pair_sin"] + PAIRS, :] * jnp.sin(angle)
-    )
-    low16 = lax.broadcasted_iota(jnp.int32, (PAIRS, 128), 1) < SEA_DEV
+    odd_side = lax.rem(me, 2) * SEA_DEV
+    even_half = lambda shape: jnp.bitwise_xor(lax.broadcasted_iota(jnp.int32, shape, 1), odd_side) < SEA_DEV
+    low16 = even_half((PAIRS, 128))
+    speed = jnp.where(even_half((1, 128)), wind, other)
+    angle = jnp.where(even_half((1, 128)), other, wind)
+
+    def paired(name):
+        rows = tab[at[name] : at[name] + PAIRS, :]
+        return jnp.where(odd_side == 0, rows, pltpu.roll(rows, SEA_DEV, 1))
+
+    toward = speed * (paired("pair_cos") * jnp.cos(angle) + paired("pair_sin") * jnp.sin(angle))
     zero16 = jnp.zeros((PAIRS, 128), jnp.float32)
     for w in range(4):
         for k in (0, 1, 2, NF + 3, NF + 4):
@@ -335,10 +390,11 @@
 
     group = 8
     per_group = half * group // PAIRS
-    finish(recv, half, recv_sem.at[0])
-
-    def arrange(h, carry):
+
+    def arrange(i, carry):
         m0, m1 = carry
+        h = lax.rem(my_x + hop(i), side)
+        finish(recv, side * cores, half, recv_sem.at[h])
         for g in (2 * h, 2 * h + 1):
             for i in range(group):
                 flat[g, half * i : half * i + half, :] = recv[g * group + i, 0:half, :]
@@ -353,7 +409,7 @@
                     rolled[w, k + 3] = b
         return m0, m1
 
-    m0, m1 = lax.fori_loop(0, n // group // 2, arrange, (zero16, zero16))
+    m0, m1 = lax.fori_loop(0, side, arrange, (zero16, zero16))
 
     def over_bins(a):
         a = jnp.sum(a, axis=0, keepdims=True)
@@ -404,16 +460,16 @@
 
     lax.fori_loop(0, n // group, add_height, 0)
 
-    exchange(back, home, half + 1, 1)
-    finish(send, half, send_sem.at[0])
-    finish(home, half + 1, recv_sem.at[1])
+    exchange(peers, back, home, half + 1, 1, recv_sem.at[side])
+    finish(send, n - 1, half, send_sem.at[0])
+    finish(home, n, half + 1, recv_sem.at[side])
 
     def unpack(g, carry):
         for u in range(2 * unroll):
             v = g * 2 * unroll + u
             a, b = home[2 * v], home[2 * v + 1]
-            moved_a[0, FAR + v] = jnp.where(low, a, pltpu.roll(b, SEA_DEV, 1))
-            moved_a[1, FAR + v] = jnp.where(low, pltpu.roll(a, SEA_DEV, 1), b)
+            moved_a[0, FAR + v] = jnp.where(low, a, b)
+            moved_a[1, FAR + v] = jnp.where(low, b, a)
         return carry
 
     lax.fori_loop(0, n * SEA_DEV // 128 // (2 * unroll), unpack, 0)
@@ -427,15 +483,26 @@
 
     lax.fori_loop(0, chunks // 4, spread, 0)
 
-    def deliver(t, u, v, tile):
-        tile = jnp.where(jnp.broadcast_to(sea_row(v), (8, 128)), lanes(tile, put, v), 0.0)
-        stage[u, pl.ds(t, half, stride=2), :] = tile[0:half]
-        if t == 0:
-            heights[pl.ds(v, 1), :] = tile[half : half + 1]
-        else:
+    def keep_apart(t, u, v, tile):
+        moved_a[t, FAR + v] = tile
+
+    near_rows(go_right, moved_b, keep_apart, False, (2, 1, 0))
+
+    def deliver(g, carry):
+        for u in range(2 * unroll):
+            v = g * 2 * unroll + u
+            sea = jnp.broadcast_to(sea_row(v), (8, 128))
+            for t in range(2):
+                tile = jnp.where(sea, lanes(moved_a[t, FAR + v], put.at[t], v), 0.0)
+                stage[u, pl.ds(t, half, stride=2), :] = tile[0:half]
+                if t == 0:
+                    heights[pl.ds(v, 1), :] = tile[half : half + 1]
+        for u in range(2 * unroll):
+            v = g * 2 * unroll + u
             out[:, pl.ds(pl.multiple_of(v * 128, 128), 128)] = stage[u, 0:bins_dev, :]
-
-    near_rows(go_right, moved_b, deliver, False, (2, 1, 0))
+        return carry
+
+    lax.fori_loop(0, chunks // (2 * unroll), deliver, 0)
 
     points = cells // n
     together = NLON // points
@@ -457,7 +524,7 @@
     height_out[...] = picked[:, 0:points]
     all_heights = jnp.sum(heights[...], axis=0, keepdims=True)
     mean_out[...] = jnp.sum(all_heights, axis=1, keepdims=True) * (1.0 / (SEA_DEV * n))
-    finish(back, half + 1, send_sem.at[1])
+    finish(back, n - 1, half + 1, send_sem.at[1])
 
 
 def solution(mesh):
@@ -471,7 +538,7 @@
         padded = chunks + 2 * (NLON // 128)
         tab, at = tables(cells // NLON)
         vmem = pl.BlockSpec(memory_space=pltpu.VMEM)
-        words = pltpu.VMEM((chunks + 2 * REACH, 128), jnp.int32)
+        words = pltpu.VMEM((2, chunks + 2 * REACH, 128), jnp.int32)
         by_freq = lambda *dims: pltpu.VMEM((*dims, PAIRS, 128), jnp.float32)
         messages = lambda count: pltpu.VMEM((count, 8, 128), jnp.float32)
         new_spectrum, height, mean = pl.pallas_call(
@@ -482,18 +549,22 @@
                 jax.ShapeDtypeStruct((1, cells // n), jnp.float32),
                 jax.ShapeDtypeStruct((1, 1), jnp.float32),
             ),
-            in_specs=[pl.BlockSpec(memory_space=pl.ANY)] + [vmem] * 4,
+            in_specs=[pl.BlockSpec(memory_space=pl.ANY)] * 5,
             out_specs=(vmem,) * 3,
             scratch_shapes=[
                 pltpu.VMEM((bins_dev, cells), jnp.float32),
+                pltpu.VMEM((chunks, 128), jnp.int32),
+                pltpu.VMEM((chunks, 128), jnp.float32),
+                pltpu.VMEM((chunks, 128), jnp.float32),
+                pltpu.VMEM(tab.shape, jnp.float32),
                 pltpu.VMEM((2, padded, 8, 128), jnp.float32),
                 pltpu.VMEM((2, padded, 8, 128), jnp.float32),
-                pltpu.VMEM((8, 16, 128), jnp.float32),
+                pltpu.VMEM((16, 16, 128), jnp.float32),
                 pltpu.VMEM((chunks + REACH, 128), jnp.int32),
                 words,
                 words,
-                pltpu.VMEM((chunks, 128), jnp.int32),
-                pltpu.VMEM((chunks, 128), jnp.int32),
+                pltpu.VMEM((2, chunks, 128), jnp.int32),
+                pltpu.VMEM((2, chunks, 128), jnp.int32),
                 pltpu.VMEM((2, chunks + 2 * FAR, 8, 128), jnp.float32),
                 pltpu.VMEM((2, chunks + 2 * FAR, 8, 128), jnp.float32),
                 messages(n),
@@ -508,9 +579,9 @@
                 by_freq(NF + 3),
                 pltpu.VMEM((chunks, 128), jnp.float32),
                 pltpu.SemaphoreType.DMA((2,)),
-                pltpu.SemaphoreType.DMA((2,)),
-                pltpu.SemaphoreType.DMA,
-                pltpu.SemaphoreType.REGULAR,
+                pltpu.SemaphoreType.DMA((side + 1,)),
+                pltpu.SemaphoreType.DMA((8,)),
+                pltpu.SemaphoreType.REGULAR((side,)),
             ],
             compiler_params=pltpu.CompilerParams(collective_id=0, has_side_effects=True),
         )(

time: 63.9 us -> 62.8 us (0.983)
  Pallas kernels: 58.7 us -> 57.6 us
    pallas_call x1, Pallas kernels: 58.7 us -> 57.6 us  [local(): pl.pallas_call(functools.partial(step_kernel, n, side, cores, at), name='...]
where the time goes in v5:
time: 62.8 us; the launch traced here: 62.6 us
  Pallas kernels  57.6 us (92%)
  local copies, waits for them, and re-layouts  2.58 us (4%)
  between operations  2.4 us (4%)
    pallas_call x1, Pallas kernels, local(): pl.pallas_call(functools.partial(step_kernel, n, side, cores, at), name='...  57.6 us
    unnamed x4, local copies, waits for them, and re-layouts  2.58 us

profile of v5, /device:TPU:513, one launch (start us, length us, event | category | flops | bytes accessed | tf_op | source)
XLA Modules:
  0.0 62.6 jit_solution(16355340929582339135)
XLA Ops:
  0.6 57.6 %wave_step.1 = (f32[12,12288]{1,0:T(8,128)}, f32[1,96]{1,0:T(1,128)}, f32[1,1]{1,0:T(1,128)}) custom-call(f32[12,12288]{1,0:T(8,128)} %x_hbm.1, s32[96,128]{1,0:T(8,128)} %bitcast.5, f32[96,128]{1,0:T(8,128)} %bitcast.6, f32[96,128]{1,0:T(8,128)} %bitcast.7, f32[272,128]{1,0:T(8,128)} %constant.2.clone.tab_hbm), custom_call_target="tpu_custom_call" | custom-call | tf_op jit(solution)/shard_map/wave_step/pallas_call | solution.py:544
  58.3 0.0 copy-start
  58.3 2.1 %copy.11 = f32[12,12288]{1,0:T(8,128)} copy(f32[12,12288]{1,0:T(8,128)} %get-tuple-element.12) | data formatting | bytes 1179648
  60.3 0.0 copy-done
  60.3 0.5 copy.12
Async XLA Ops:
  58.3 2.1 %copy-start = (f32[1,96]{1,0:T(1,128)S(1)}, f32[1,96]{1,0:T(1,128)}, u32[]{:S(2)}) copy-start(f32[1,96]{1,0:T(1,128)} %get-tuple-element.7) | copy-start | bytes 1156

commit v6 on v5

--- a/solution.py
+++ b/solution.py
@@ -113,13 +113,23 @@
 
         def far_row(i, carry):
             py = lax.rem(my_y + hop(i), side)
-            pl.semaphore_wait(column_sem.at[py], 1)
-            row_of(py, side)
+
+            @pl.when(py != 0)
+            def _():
+                pl.semaphore_wait(column_sem.at[py], 1)
+                row_of(py, side)
+
             return carry
 
         lax.fori_loop(0, side - 1, far_row, 0)
         row_of(my_y, side - 1)
         own_chip(act)
+
+        @pl.when(my_y != 0)
+        def _():
+            pl.semaphore_wait(column_sem.at[0], 1)
+            row_of(0, side)
+
 
     barrier = pltpu.get_barrier_semaphore()
 

time: 62.8 us -> 59.8 us (0.952)
  Pallas kernels: 57.6 us -> 54.7 us
    pallas_call x1, Pallas kernels: 57.6 us -> 54.7 us  [local(): pl.pallas_call(functools.partial(step_kernel, n, side, cores, at), name='...]
where the time goes in v6:
time: 59.8 us; the launch traced here: 59.7 us
  Pallas kernels  54.7 us (91%)
  local copies, waits for them, and re-layouts  2.58 us (4%)
  between operations  2.4 us (4%)
    pallas_call x1, Pallas kernels, local(): pl.pallas_call(functools.partial(step_kernel, n, side, cores, at), name='...  54.7 us
    unnamed x4, local copies, waits for them, and re-layouts  2.58 us

profile of v6, /device:TPU:513, one launch (start us, length us, event | category | flops | bytes accessed | tf_op | source)
XLA Modules:
  0.0 59.7 jit_solution(13935439506555684772)
XLA Ops:
  0.6 54.7 %wave_step.1 = (f32[12,12288]{1,0:T(8,128)}, f32[1,96]{1,0:T(1,128)}, f32[1,1]{1,0:T(1,128)}) custom-call(f32[12,12288]{1,0:T(8,128)} %x_hbm.1, s32[96,128]{1,0:T(8,128)} %bitcast.5, f32[96,128]{1,0:T(8,128)} %bitcast.6, f32[96,128]{1,0:T(8,128)} %bitcast.7, f32[272,128]{1,0:T(8,128)} %constant.2.clone.tab_hbm), custom_call_target="tpu_custom_call" | custom-call | tf_op jit(solution)/shard_map/wave_step/pallas_call | solution.py:554
  55.3 0.0 copy-start
  55.3 2.1 %copy.11 = f32[12,12288]{1,0:T(8,128)} copy(f32[12,12288]{1,0:T(8,128)} %get-tuple-element.12) | data formatting | bytes 1179648
  57.4 0.0 copy-done
  57.4 0.5 copy.12
Async XLA Ops:
  55.3 2.1 %copy-start = (f32[1,96]{1,0:T(1,128)S(1)}, f32[1,96]{1,0:T(1,128)}, u32[]{:S(2)}) copy-start(f32[1,96]{1,0:T(1,128)} %get-tuple-element.7) | copy-start | bytes 1156

commit v7 on v6

--- a/solution.py
+++ b/solution.py
@@ -19,6 +19,8 @@
 PAIRS = ND // 2
 ROW_STEPS = 6
 REACH = 32
+UNROLL = 8
+VMEM_BYTES = 24 * 1024 * 1024
 FAR = 56
 
 
@@ -44,12 +46,59 @@
     return np.concatenate(rows).astype(np.float32), at
 
 
+def word_of(words, v):
+    return jnp.broadcast_to(words[pl.ds(REACH + v, 1), :], (8, 128))
+
+
+def has(word, i):
+    return jnp.bitwise_and(word, 1 << i) != 0
+
+
+def lanes(tile, index, v):
+    index = jnp.broadcast_to(index[pl.ds(v, 1), :], (8, 128))
+    return jnp.take_along_axis(tile, index, axis=1, mode="promise_in_bounds")
+
+
+def near_rows(chunks, words, src, emit, toward_end, bit_order):
+    way = 1 if toward_end else -1
+
+    def block(g, carry):
+        first = g * UNROLL
+        span = [first + way * u if toward_end else first + UNROLL - 1 - u for u in range(UNROLL + 7)]
+        for t in range(2):
+            word = [word_of(words.at[t], v) for v in span]
+            cur = [src[t, FAR + v] for v in span]
+            for b in bit_order:
+                d = 1 << b
+                cur = [
+                    jnp.where(has(word[u], b), cur[u + d], cur[u])
+                    for u in range(len(cur) - d)
+                ]
+            for u in range(UNROLL):
+                emit(t, u, span[u], cur[u])
+        return carry
+
+    lax.fori_loop(0, chunks // UNROLL, block, 0)
+
+
+def far_rows(words, src, t, v, way, bit_order):
+    def value(v, order):
+        if not order:
+            return src[t, FAR + v]
+        d = way * (1 << order[-1])
+        return jnp.where(
+            has(word_of(words.at[t], v), order[-1]), value(v + d, order[:-1]), value(v, order[:-1])
+        )
+
+    return value(v, bit_order)
+
+
 def step_kernel(
     n, side, cores, at,
     x_hbm, mask_hbm, speed_hbm, angle_hbm, tab_hbm,
-    out, height_out, mean_out,
-    x, mask2d, speed2d, angle2d, tab, field_a, field_b, stage, shifts, go_left, go_right, pick, put, moved_a, moved_b,
-    send, recv, back, home, flat, energy, rolled, own, low_part, high_part, heights,
+    home, go_right, put,
+    x, mask2d, speed2d, angle2d, tab, field_a, field_b, stage, shifts, go_left, pick, moved_a, moved_b,
+    send, recv, back, flat, energy, rolled, own, low_part, high_part,
     send_sem, recv_sem, load_sem, column_sem,
 ):
     bins_dev, cells = x.shape
@@ -240,10 +289,6 @@
         return lax.fori_loop(part * per_part, (part + 1) * per_part, split_bins, carry)
 
     lax.fori_loop(0, parts, split_part, 0)
-
-    def lanes(tile, index, v):
-        index = jnp.broadcast_to(index[pl.ds(v, 1), :], (8, 128))
-        return jnp.take_along_axis(tile, index, axis=1, mode="promise_in_bounds")
 
     for s in range(SUBSTEPS):
         src, dst = (field_a, field_b) if s % 2 == 0 else (field_b, field_a)
@@ -290,60 +335,21 @@
     pl.semaphore_wait(barrier, side * cores + side - 2)
     call_column(column_sem.at[my_y])
 
-    unroll = 8
-
-    def word_of(words, v):
-        return jnp.broadcast_to(words[pl.ds(REACH + v, 1), :], (8, 128))
-
-    def has(word, i):
-        return jnp.bitwise_and(word, 1 << i) != 0
-
-    def near_rows(words, src, emit, toward_end, bit_order):
-        way = 1 if toward_end else -1
-
-        def block(g, carry):
-            first = g * unroll
-            span = [first + way * u if toward_end else first + unroll - 1 - u for u in range(unroll + 7)]
-            for t in range(2):
-                word = [word_of(words.at[t], v) for v in span]
-                cur = [src[t, FAR + v] for v in span]
-                for b in bit_order:
-                    d = 1 << b
-                    cur = [
-                        jnp.where(has(word[u], b), cur[u + d], cur[u])
-                        for u in range(len(cur) - d)
-                    ]
-                for u in range(unroll):
-                    emit(t, u, span[u], cur[u])
-            return carry
-
-        lax.fori_loop(0, chunks // unroll, block, 0)
-
-    def far_rows(words, src, t, v, way, bit_order):
-        def value(v, order):
-            if not order:
-                return src[t, FAR + v]
-            d = way * (1 << order[-1])
-            return jnp.where(
-                has(word_of(words.at[t], v), order[-1]), value(v + d, order[:-1]), value(v, order[:-1])
-            )
-
-        return value(v, bit_order)
 
     def keep_near(t, u, v, tile):
         moved_b[t, FAR + v] = tile
 
-    near_rows(go_left, moved_a, keep_near, True, (0, 1, 2))
+    near_rows(chunks, go_left, moved_a, keep_near, True, (0, 1, 2))
 
     def pack(g, carry):
-        for u in range(unroll):
-            v = g * unroll + u
+        for u in range(UNROLL):
+            v = g * UNROLL + u
             even, odd = (far_rows(go_left, moved_b, t, v, 1, (3, 4, 5)) for t in range(2))
             send[2 * v] = jnp.where(low, even, odd)
             send[2 * v + 1] = jnp.where(low, odd, even)
         return carry
 
-    lax.fori_loop(0, n * SEA_DEV // 128 // unroll, pack, 0)
+    lax.fori_loop(0, n * SEA_DEV // 128 // UNROLL, pack, 0)
 
 
     def exchange(visit, src, dst, rows, k, arrival):
@@ -473,16 +479,32 @@
     exchange(peers, back, home, half + 1, 1, recv_sem.at[side])
     finish(send, n - 1, half, send_sem.at[0])
     finish(home, n, half + 1, recv_sem.at[side])
+    finish(back, n - 1, half + 1, send_sem.at[1])
+
+
+def unpack_kernel(
+    n, bins_dev,
+    home, go_right, put, mask2d,
+    out, height_out, mean_out,
+    moved_a, moved_b, stage, heights,
+):
+    chunks = mask2d.shape[0]
+    half = bins_dev // 2
+    cells = chunks * 128
+    per_row = NLON // 128
+    me = lax.axis_index("spec")
+    lane = lax.broadcasted_iota(jnp.int32, (8, 128), 1)
+    low = lane < SEA_DEV
 
     def unpack(g, carry):
-        for u in range(2 * unroll):
-            v = g * 2 * unroll + u
+        for u in range(2 * UNROLL):
+            v = g * 2 * UNROLL + u
             a, b = home[2 * v], home[2 * v + 1]
             moved_a[0, FAR + v] = jnp.where(low, a, b)
             moved_a[1, FAR + v] = jnp.where(low, b, a)
         return carry
 
-    lax.fori_loop(0, n * SEA_DEV // 128 // (2 * unroll), unpack, 0)
+    lax.fori_loop(0, n * SEA_DEV // 128 // (2 * UNROLL), unpack, 0)
 
     def spread(g, carry):
         for u in range(4):
@@ -496,23 +518,23 @@
     def keep_apart(t, u, v, tile):
         moved_a[t, FAR + v] = tile
 
-    near_rows(go_right, moved_b, keep_apart, False, (2, 1, 0))
+    near_rows(chunks, go_right, moved_b, keep_apart, False, (2, 1, 0))
 
     def deliver(g, carry):
-        for u in range(2 * unroll):
-            v = g * 2 * unroll + u
-            sea = jnp.broadcast_to(sea_row(v), (8, 128))
+        for u in range(2 * UNROLL):
+            v = g * 2 * UNROLL + u
+            sea = jnp.broadcast_to(mask2d[pl.ds(v, 1), :] != 0, (8, 128))
             for t in range(2):
                 tile = jnp.where(sea, lanes(moved_a[t, FAR + v], put.at[t], v), 0.0)
                 stage[u, pl.ds(t, half, stride=2), :] = tile[0:half]
                 if t == 0:
                     heights[pl.ds(v, 1), :] = tile[half : half + 1]
-        for u in range(2 * unroll):
-            v = g * 2 * unroll + u
+        for u in range(2 * UNROLL):
+            v = g * 2 * UNROLL + u
             out[:, pl.ds(pl.multiple_of(v * 128, 128), 128)] = stage[u, 0:bins_dev, :]
         return carry
 
-    lax.fori_loop(0, chunks // (2 * unroll), deliver, 0)
+    lax.fori_loop(0, chunks // (2 * UNROLL), deliver, 0)
 
     points = cells // n
     together = NLON // points
@@ -534,7 +556,6 @@
     height_out[...] = picked[:, 0:points]
     all_heights = jnp.sum(heights[...], axis=0, keepdims=True)
     mean_out[...] = jnp.sum(all_heights, axis=1, keepdims=True) * (1.0 / (SEA_DEV * n))
-    finish(back, n - 1, half + 1, send_sem.at[1])
 
 
 def solution(mesh):
@@ -551,15 +572,15 @@
         words = pltpu.VMEM((2, chunks + 2 * REACH, 128), jnp.int32)
         by_freq = lambda *dims: pltpu.VMEM((*dims, PAIRS, 128), jnp.float32)
         messages = lambda count: pltpu.VMEM((count, 8, 128), jnp.float32)
-        new_spectrum, height, mean = pl.pallas_call(
+        home, go_right, put = pl.pallas_call(
             functools.partial(step_kernel, n, side, cores, at),
             name="wave_step",
             out_shape=(
-                jax.ShapeDtypeStruct((bins_dev, cells), jnp.float32),
-                jax.ShapeDtypeStruct((1, cells // n), jnp.float32),
-                jax.ShapeDtypeStruct((1, 1), jnp.float32),
+                jax.ShapeDtypeStruct((n, 8, 128), jnp.float32),
+                jax.ShapeDtypeStruct((2, chunks + 2 * REACH, 128), jnp.int32),
+                jax.ShapeDtypeStruct((2, chunks, 128), jnp.int32),
             ),
-            in_specs=[pl.BlockSpec(memory_space=pl.ANY)] * 5,
+            in_specs=[pl.BlockSpec(memory_space=pltpu.HBM)] * 5,
             out_specs=(vmem,) * 3,
             scratch_shapes=[
                 pltpu.VMEM((bins_dev, cells), jnp.float32),
@@ -569,15 +590,12 @@
                 pltpu.VMEM(tab.shape, jnp.float32),
                 pltpu.VMEM((2, padded, 8, 128), jnp.float32),
                 pltpu.VMEM((2, padded, 8, 128), jnp.float32),
-                pltpu.VMEM((16, 16, 128), jnp.float32),
+                pltpu.VMEM((8, 16, 128), jnp.float32),
                 pltpu.VMEM((chunks + REACH, 128), jnp.int32),
                 words,
-                words,
-                pltpu.VMEM((2, chunks, 128), jnp.int32),
                 pltpu.VMEM((2, chunks, 128), jnp.int32),
                 pltpu.VMEM((2, chunks + 2 * FAR, 8, 128), jnp.float32),
                 pltpu.VMEM((2, chunks + 2 * FAR, 8, 128), jnp.float32),
-                messages(n),
                 messages(n),
                 messages(n),
                 messages(n),
@@ -587,20 +605,45 @@
                 by_freq(NF),
                 by_freq(NF + 2),
                 by_freq(NF + 3),
-                pltpu.VMEM((chunks, 128), jnp.float32),
                 pltpu.SemaphoreType.DMA((2,)),
                 pltpu.SemaphoreType.DMA((side + 1,)),
                 pltpu.SemaphoreType.DMA((8,)),
                 pltpu.SemaphoreType.REGULAR((side,)),
             ],
-            compiler_params=pltpu.CompilerParams(collective_id=0, has_side_effects=True),
+            compiler_params=pltpu.CompilerParams(
+                collective_id=0, has_side_effects=True, vmem_limit_bytes=VMEM_BYTES
+            ),
         )(
-            spectrum,
-            sea_mask.reshape(chunks, 128),
-            wind_speed.reshape(chunks, 128),
-            wind_angle.reshape(chunks, 128),
-            tab,
+            *(
+                pltpu.with_memory_space_constraint(a, pltpu.HBM)
+                for a in (
+                    spectrum,
+                    sea_mask.reshape(chunks, 128),
+                    wind_speed.reshape(chunks, 128),
+                    wind_angle.reshape(chunks, 128),
+                    jnp.asarray(tab),
+                )
+            )
         )
+        moved = pltpu.VMEM((2, chunks + 2 * FAR, 8, 128), jnp.float32)
+        new_spectrum, height, mean = pl.pallas_call(
+            functools.partial(unpack_kernel, n, bins_dev),
+            name="unpack",
+            out_shape=(
+                jax.ShapeDtypeStruct((bins_dev, cells), jnp.float32),
+                jax.ShapeDtypeStruct((1, cells // n), jnp.float32),
+                jax.ShapeDtypeStruct((1, 1), jnp.float32),
+            ),
+            in_specs=[vmem] * 4,
+            out_specs=(vmem,) * 3,
+            scratch_shapes=[
+                moved,
+                moved,
+                pltpu.VMEM((16, 16, 128), jnp.float32),
+                pltpu.VMEM((chunks, 128), jnp.float32),
+            ],
+            compiler_params=pltpu.CompilerParams(vmem_limit_bytes=VMEM_BYTES),
+        )(home, go_right, put, sea_mask.reshape(chunks, 128))
         return new_spectrum, height.reshape(-1), mean.reshape(1)
 
     return jax.shard_map(

time: 59.8 us -> 55.4 us (0.926)
  local copies, waits for them, and re-layouts: 2.58 us -> 0.01 us
  between operations: 2.4 us -> 0.65 us
    pallas_call x1, Pallas kernels: 54.7 us -> 51.5 us  [local(): pl.pallas_call(functools.partial(step_kernel, n, side, cores, at), name='...]
    pallas_call x0 -> x1, Pallas kernels: none -> 3.07 us  [local(): pl.pallas_call(functools.partial(unpack_kernel, n, bins_dev), name='unpac...]
    unnamed x4 -> x2, local copies, waits for them, and re-layouts: 2.58 us -> 0.01 us
where the time goes in v7:
time: 55.4 us; the launch traced here: 55.3 us
  Pallas kernels  54.6 us (99%)
  between operations  0.65 us (1%)
    pallas_call x1, Pallas kernels, local(): pl.pallas_call(functools.partial(step_kernel, n, side, cores, at), name='...  51.5 us
    pallas_call x1, Pallas kernels, local(): pl.pallas_call(functools.partial(unpack_kernel, n, bins_dev), name='unpac...  3.07 us

profile of v7, /device:TPU:513, one launch (start us, length us, event | category | flops | bytes accessed | tf_op | source)
XLA Modules:
  0.0 55.3 jit_solution(16929781462976082445)
XLA Ops:
  0.6 0.0 copy-start
  0.6 51.5 %wave_step.1 = (f32[128,8,128]{2,1,0:T(8,128)S(1)}, s32[2,160,128]{2,1,0:T(8,128)S(1)}, s32[2,96,128]{2,1,0:T(8,128)S(1)}) custom-call(f32[12,12288]{1,0:T(8,128)} %x_hbm.1, s32[96,128]{1,0:T(8,128)} %bitcast.5, f32[96,128]{1,0:T(8,128)} %bitcast.7, f32[96,128]{1,0:T(8,128)} %bitcast.8, f32[272,128]{1,0:T(8,128)} %constant.2.clone.tab_hbm), custom_call_target="tpu_custom_call" | custom-call | tf_op jit(solution)/shard_map/wave_step/pallas_call | solution.py:575
  52.2 0.0 copy-done
  52.2 3.1 %unpack.1 = (f32[12,12288]{1,0:T(8,128)}, f32[1,96]{1,0:T(1,128)}, f32[1,1]{1,0:T(1,128)}) custom-call(f32[128,8,128]{2,1,0:T(8,128)S(1)} %get-tuple-element.9.home, s32[2,160,128]{2,1,0:T(8,128)S(1)} %get-tuple-element.10.go_right, s32[2,96,128]{2,1,0:T(8,128)S(1)} %get-tuple-element.11.put, s32[96,128]{1,0:T(8,128)S(1)} %bitcast.6), custom_call_target="tpu_custom_call" | custom-call | tf_op jit(solution)/shard_map/unpack/pallas_call | solution.py:629
Async XLA Ops:
  0.6 51.6 %copy-start = (s32[12288]{0:T(1024)S(1)}, s32[12288]{0:T(1024)}, u32[]{:S(2)}) copy-start(s32[12288]{0:T(1024)} %param.6) | copy-start | bytes 147460

commit v8 on v7

--- a/solution.py
+++ b/solution.py
@@ -97,9 +97,9 @@
     n, side, cores, at,
     x_hbm, mask_hbm, speed_hbm, angle_hbm, tab_hbm,
     home, go_right, put,
-    x, mask2d, speed2d, angle2d, tab, field_a, field_b, stage, shifts, go_left, pick, moved_a, moved_b,
+    x, mask2d, sea_float, speed2d, angle2d, tab, field_a, field_b, stage, shifts, go_left, pick, moved_a, moved_b,
     send, recv, back, flat, energy, rolled, own, low_part, high_part,
-    send_sem, recv_sem, load_sem, column_sem,
+    send_sem, recv_sem, load_sem, column_sem, first_sem,
 ):
     bins_dev, cells = x.shape
     half = bins_dev // 2
@@ -128,75 +128,125 @@
     for copy in small[1:]:
         copy.start()
 
+    def wrap(a):
+        return jnp.bitwise_and(a, side - 1) if side & (side - 1) == 0 else lax.rem(a, side)
+
     def hop(u):
-        return side // 2 + jnp.where(lax.rem(u, 2) == 0, u // 2, -((u + 1) // 2))
+        return side // 2 + (1 - 2 * jnp.bitwise_and(u, 1)) * jnp.right_shift(u + 1, 1)
 
     def both_cores(act, px, py):
         first = (px * side + py) * cores
         act(first + my_c)
         for c in range(1, cores):
-            act(first + lax.rem(my_c + c, cores))
+            act(first + jnp.where(my_c + c >= cores, my_c + c - cores, my_c + c))
 
     def own_chip(act):
         for c in range(1, cores):
             act(me - my_c + lax.rem(my_c + c, cores))
 
-    def peers(act):
+    def peers(act, rows=side):
         def diagonal(s, carry):
             def one(u, inner):
-                both_cores(act, lax.rem(my_x + hop(u), side), lax.rem(my_y + hop(s - u), side))
+                both_cores(act, wrap(my_x + hop(u)), wrap(my_y + hop(s - u)))
                 return inner
 
-            return lax.fori_loop(jnp.maximum(0, s - side + 1), jnp.minimum(side - 1, s) + 1, one, carry)
-
-        lax.fori_loop(0, 2 * side - 2, diagonal, 0)
+            return lax.fori_loop(jnp.maximum(0, s - rows + 1), jnp.minimum(side - 1, s) + 1, one, carry)
+
+        lax.fori_loop(0, side + rows - 2 + (rows < side), diagonal, 0)
+        if rows == side:
+            own_chip(act)
+
+    is_first = me == 0
+    below_first = jnp.logical_and(jnp.logical_and(my_x == 0, my_c == 0), my_y != 0)
+
+    def signal(semaphore, to):
+        pl.semaphore_signal(semaphore, inc=1, device_id={"spec": to}, device_id_type=MESH)
+
+    def down_column(act):
+        def one(u, carry):
+            act((my_x * side + wrap(my_y + hop(u))) * cores + my_c)
+            return carry
+
+        lax.fori_loop(0, side - 1, one, 0)
+
+    def along_row(act):
+        def one(u, carry):
+            both_cores(act, wrap(my_x + hop(u)), my_y)
+            return carry
+
+        lax.fori_loop(0, side - 1, one, 0)
         own_chip(act)
 
-    def peers_by_row(act):
-        def row_of(py, count):
-            def one(u, inner):
-                both_cores(act, lax.rem(my_x + hop(u), side), py)
-                return inner
-
-            lax.fori_loop(0, count, one, 0)
-
-        def far_row(i, carry):
-            py = lax.rem(my_y + hop(i), side)
-
-            @pl.when(py != 0)
+    def peers_but_late(act):
+        def but_first(to):
+            @pl.when(to != 0)
             def _():
-                pl.semaphore_wait(column_sem.at[py], 1)
-                row_of(py, side)
-
-            return carry
-
-        lax.fori_loop(0, side - 1, far_row, 0)
-        row_of(my_y, side - 1)
-        own_chip(act)
-
-        @pl.when(my_y != 0)
+                act(to)
+
+        along_row(but_first)
+
+        @pl.when(jnp.logical_not(is_first))
         def _():
-            pl.semaphore_wait(column_sem.at[0], 1)
-            row_of(0, side)
-
+            def row_in(i, carry):
+                pl.semaphore_wait(column_sem.at[wrap(my_y + i)], 1)
+                return carry
+
+            @pl.when(jnp.logical_not(below_first))
+            def _():
+                lax.fori_loop(1, side, row_in, 0)
+
+            @pl.when(me == 1)
+            def _():
+                down_column(lambda to: signal(column_sem.at[0], to - 1))
+
+            @pl.when(below_first)
+            def _():
+                lax.fori_loop(1, side, row_in, 0)
+
+        peers(but_first, side - 1)
+
+        @pl.when(jnp.logical_not(is_first))
+        def _():
+            pl.semaphore_wait(first_sem, 1)
+
+            @pl.when(my_y == 0)
+            def _():
+                down_column(lambda to: signal(first_sem, to))
+
+            act(0)
 
     barrier = pltpu.get_barrier_semaphore()
 
-    def call_row(i, carry):
-        to = (lax.rem(my_x + i // cores, side) * side + my_y) * cores + lax.rem(my_c + lax.rem(i, cores), cores)
-        pl.semaphore_signal(barrier, inc=1, device_id={"spec": to}, device_id_type=MESH)
-        return carry
-
-    def call_column(semaphore):
-        def one(i, carry):
-            to = (my_x * side + lax.rem(my_y + i, side)) * cores + my_c
-            pl.semaphore_signal(semaphore, inc=1, device_id={"spec": to}, device_id_type=MESH)
-            return carry
-
-        lax.fori_loop(1, side, one, 0)
-
-    lax.fori_loop(1, side * cores, call_row, 0)
-    call_column(barrier)
+    @pl.when(jnp.logical_not(is_first))
+    def _():
+        along_row(lambda to: signal(barrier, to))
+        down_column(lambda to: signal(barrier, to))
+
+    def entered():
+        called = side * cores + side - 2
+
+        @pl.when(is_first)
+        def _():
+            pl.semaphore_wait(barrier, called + side - 1)
+            along_row(lambda to: signal(first_sem, to))
+            down_column(lambda to: signal(first_sem, to))
+
+        @pl.when(jnp.logical_not(is_first))
+        def _():
+            with_first = jnp.logical_or(my_y == 0, below_first)
+            pl.semaphore_wait(barrier, called - jnp.where(with_first, 1, 0))
+
+            def complete(to):
+                @pl.when(to == 0)
+                def _():
+                    signal(barrier, to)
+
+                @pl.when(to != 0)
+                def _():
+                    signal(column_sem.at[my_y], to)
+
+            down_column(complete)
+
     small[0].wait()
 
     lane = lax.broadcasted_iota(jnp.int32, (8, 128), 1)
@@ -204,6 +254,7 @@
     low = lane < SEA_DEV
 
     is_sea = mask2d[...] != 0
+    sea_float[...] = mask2d[...].astype(jnp.float32)
     land = jnp.where(is_sea, 0.0, 1.0).astype(jnp.bfloat16)
     earlier = (
         lax.broadcasted_iota(jnp.int32, (128, 128), 0) < lax.broadcasted_iota(jnp.int32, (128, 128), 1)
@@ -271,14 +322,11 @@
         cs.append(jnp.maximum(ay, 0.0))
         cn.append(-jnp.minimum(ay, 0.0))
 
-    def sea_row(v):
-        return mask2d[pl.ds(v, 1), :] != 0
-
     def split_bins(g, carry):
         for u in range(8):
             v = g * 8 + u
             cols = pl.ds(pl.multiple_of(v * 128, 128), 128)
-            stage[u, 0:bins_dev, :] = jnp.where(sea_row(v), x[:, cols], 0.0)
+            stage[u, 0:bins_dev, :] = x[:, cols] * sea_float[pl.ds(v, 1), :]
             for t in range(2):
                 field_a[t, pad + v, 0:half, :] = stage[u, pl.ds(t, half, stride=2), :]
         return carry
@@ -295,15 +343,9 @@
 
         def advance(g, to_go, src=src, dst=dst, s=s):
             if s == 0:
-                to_go = close_up(g, to_go)
-            else:
-                behind = jnp.maximum(g - 1, 0) * 4 * per_row
-                for u in range(4 * per_row):
-                    for t in range(2):
-                        v = behind + u
-                        moved_a[t, FAR + v] = lanes(dst[t, pad + v], pick.at[t], v)
-            for ru in range(4):
-                r = jnp.minimum(g, lat_count // 4 - 1) * 4 + ru
+                to_go = close_up(2 * g + 1, close_up(2 * g, to_go))
+            for ru in range(8):
+                r = g * 8 + ru
                 widen = tab[pl.ds(at["widen"] + r, 1), :]
                 first = pad + r * per_row
                 for t in range(2):
@@ -322,18 +364,26 @@
                         )
                         v = first + q - pad
                         if s < SUBSTEPS - 1:
-                            dst[t, first + q] = jnp.where(sea_row(v), new, 0.0)
+                            dst[t, first + q] = new * sea_float[pl.ds(v, 1), :]
                         else:
                             wind = (speed2d, angle2d)[t][pl.ds(v, 1), :]
                             dst[t, first + q] = jnp.where(row == half, wind, new)
             return to_go
 
-        to_go = lax.fori_loop(0, lat_count // 4 + min(s, 1), advance, to_go)
+        to_go = lax.fori_loop(0, lat_count // 8, advance, to_go)
         if s == 0:
             plan_rows(to_go)
-
-    pl.semaphore_wait(barrier, side * cores + side - 2)
-    call_column(column_sem.at[my_y])
+    final = field_a if SUBSTEPS % 2 == 0 else field_b
+    entered()
+
+    def to_lanes(g, carry):
+        for u in range(2 * UNROLL):
+            v = g * 2 * UNROLL + u
+            for t in range(2):
+                moved_a[t, FAR + v] = lanes(final[t, pad + v], pick.at[t], v)
+        return carry
+
+    lax.fori_loop(0, chunks // (2 * UNROLL), to_lanes, 0)
 
 
     def keep_near(t, u, v, tile):
@@ -370,7 +420,7 @@
         part = ref.at[pl.ds(0, count), pl.ds(0, rows)]
         pltpu.make_async_copy(part, part, sem).wait()
 
-    exchange(peers_by_row, send, recv, half, 0, recv_sem.at[my_x])
+    exchange(peers_but_late, send, recv, half, 0, recv_sem.at[my_x])
 
     wind = send[me][half : half + 1, :]
     other = pltpu.roll(wind, SEA_DEV, 1)
@@ -409,7 +459,7 @@
 
     def arrange(i, carry):
         m0, m1 = carry
-        h = lax.rem(my_x + hop(i), side)
+        h = lax.rem(i + 1, side)
         finish(recv, side * cores, half, recv_sem.at[h])
         for g in (2 * h, 2 * h + 1):
             for i in range(group):
@@ -587,6 +637,7 @@
                 pltpu.VMEM((chunks, 128), jnp.int32),
                 pltpu.VMEM((chunks, 128), jnp.float32),
                 pltpu.VMEM((chunks, 128), jnp.float32),
+                pltpu.VMEM((chunks, 128), jnp.float32),
                 pltpu.VMEM(tab.shape, jnp.float32),
                 pltpu.VMEM((2, padded, 8, 128), jnp.float32),
                 pltpu.VMEM((2, padded, 8, 128), jnp.float32),
@@ -609,6 +660,7 @@
                 pltpu.SemaphoreType.DMA((side + 1,)),
                 pltpu.SemaphoreType.DMA((8,)),
                 pltpu.SemaphoreType.REGULAR((side,)),
+                pltpu.SemaphoreType.REGULAR,
             ],
             compiler_params=pltpu.CompilerParams(
                 collective_id=0, has_side_effects=True, vmem_limit_bytes=VMEM_BYTES

time: 55.4 us -> 53.6 us (0.968)
  Pallas kernels: 54.6 us -> 52.9 us
    pallas_call x1, Pallas kernels: 51.5 us -> 49.8 us  [local(): pl.pallas_call(functools.partial(step_kernel, n, side, cores, at), name='...]
where the time goes in v8:
time: 53.6 us; the launch traced here: 53.5 us
  Pallas kernels  52.9 us (99%)
  between operations  0.65 us (1%)
    pallas_call x1, Pallas kernels, local(): pl.pallas_call(functools.partial(step_kernel, n, side, cores, at), name='...  49.8 us
    pallas_call x1, Pallas kernels, local(): pl.pallas_call(functools.partial(unpack_kernel, n, bins_dev), name='unpac...  3.07 us

profile of v8, /device:TPU:513, one launch (start us, length us, event | category | flops | bytes accessed | tf_op | source)
XLA Modules:
  0.0 53.5 jit_solution(3823617071341722449)
XLA Ops:
  0.6 0.0 copy-start
  0.6 49.8 %wave_step.1 = (f32[128,8,128]{2,1,0:T(8,128)S(1)}, s32[2,160,128]{2,1,0:T(8,128)S(1)}, s32[2,96,128]{2,1,0:T(8,128)S(1)}) custom-call(f32[12,12288]{1,0:T(8,128)} %x_hbm.1, s32[96,128]{1,0:T(8,128)} %bitcast.5, f32[96,128]{1,0:T(8,128)} %bitcast.7, f32[96,128]{1,0:T(8,128)} %bitcast.8, f32[272,128]{1,0:T(8,128)} %constant.2.clone.tab_hbm), custom_call_target="tpu_custom_call" | custom-call | tf_op jit(solution)/shard_map/wave_step/pallas_call | solution.py:625
  50.4 0.0 copy-done
  50.5 3.1 %unpack.1 = (f32[12,12288]{1,0:T(8,128)}, f32[1,96]{1,0:T(1,128)}, f32[1,1]{1,0:T(1,128)}) custom-call(f32[128,8,128]{2,1,0:T(8,128)S(1)} %get-tuple-element.9.home, s32[2,160,128]{2,1,0:T(8,128)S(1)} %get-tuple-element.10.go_right, s32[2,96,128]{2,1,0:T(8,128)S(1)} %get-tuple-element.11.put, s32[96,128]{1,0:T(8,128)S(1)} %bitcast.6), custom_call_target="tpu_custom_call" | custom-call | tf_op jit(solution)/shard_map/unpack/pallas_call | solution.py:681
Async XLA Ops:
  0.6 49.8 %copy-start = (s32[12288]{0:T(1024)S(1)}, s32[12288]{0:T(1024)}, u32[]{:S(2)}) copy-start(s32[12288]{0:T(1024)} %param.6) | copy-start | bytes 147460

commit v9 on v8

--- a/solution.py
+++ b/solution.py
@@ -46,6 +46,18 @@
     return np.concatenate(rows).astype(np.float32), at
 
 
+def chip_order(side):
+    hops = lambda d: min(d, side - d)
+    way = lambda d: (d > 0) - 2 * (d > side // 2)
+    chips = [(x, y) for x in range(side) for y in range(side)][1:]
+    chips.sort(key=lambda o: (-(hops(o[0]) + hops(o[1])), 3 * o[0] + 5 * o[1]))
+    kinds = {}
+    for o in chips:
+        kinds.setdefault((way(o[0]), way(o[1])), []).append(o)
+    placed = [((i + 0.5) / len(k), o) for k in kinds.values() for i, o in enumerate(k)]
+    return [o for _, o in sorted(placed, key=lambda p: p[0])]
+
+
 def word_of(words, v):
     return jnp.broadcast_to(words[pl.ds(REACH + v, 1), :], (8, 128))
 
@@ -99,7 +111,7 @@
     home, go_right, put,
     x, mask2d, sea_float, speed2d, angle2d, tab, field_a, field_b, stage, shifts, go_left, pick, moved_a, moved_b,
     send, recv, back, flat, energy, rolled, own, low_part, high_part,
-    send_sem, recv_sem, load_sem, column_sem, first_sem,
+    order, send_sem, recv_sem, load_sem, column_sem, first_sem,
 ):
     bins_dev, cells = x.shape
     half = bins_dev // 2
@@ -144,19 +156,18 @@
         for c in range(1, cores):
             act(me - my_c + lax.rem(my_c + c, cores))
 
-    def peers(act, rows=side):
-        def diagonal(s, carry):
-            def one(u, inner):
-                both_cores(act, wrap(my_x + hop(u)), wrap(my_y + hop(s - u)))
-                return inner
-
-            return lax.fori_loop(jnp.maximum(0, s - rows + 1), jnp.minimum(side - 1, s) + 1, one, carry)
-
-        lax.fori_loop(0, side + rows - 2 + (rows < side), diagonal, 0)
-        if rows == side:
-            own_chip(act)
+    chips = chip_order(side)
+    other_rows = [o for o in chips if o[1] != 0]
+
+    def peers(act, which, count):
+        def chip(i, carry):
+            both_cores(act, wrap(my_x + order[2 * which, i]), wrap(my_y + order[2 * which + 1, i]))
+            return carry
+
+        lax.fori_loop(0, count, chip, 0)
 
     is_first = me == 0
+    is_second = me == 1
     below_first = jnp.logical_and(jnp.logical_and(my_x == 0, my_c == 0), my_y != 0)
 
     def signal(semaphore, to):
@@ -169,21 +180,16 @@
 
         lax.fori_loop(0, side - 1, one, 0)
 
-    def along_row(act):
+    def along_row(act, own=None):
         def one(u, carry):
             both_cores(act, wrap(my_x + hop(u)), my_y)
             return carry
 
         lax.fori_loop(0, side - 1, one, 0)
-        own_chip(act)
-
-    def peers_but_late(act):
-        def but_first(to):
-            @pl.when(to != 0)
-            def _():
-                act(to)
-
-        along_row(but_first)
+        own_chip(act if own is None else own)
+
+    def peers_as_known(act, own):
+        along_row(act, own)
 
         @pl.when(jnp.logical_not(is_first))
         def _():
@@ -195,7 +201,7 @@
             def _():
                 lax.fori_loop(1, side, row_in, 0)
 
-            @pl.when(me == 1)
+            @pl.when(is_second)
             def _():
                 down_column(lambda to: signal(column_sem.at[0], to - 1))
 
@@ -203,17 +209,7 @@
             def _():
                 lax.fori_loop(1, side, row_in, 0)
 
-        peers(but_first, side - 1)
-
-        @pl.when(jnp.logical_not(is_first))
-        def _():
-            pl.semaphore_wait(first_sem, 1)
-
-            @pl.when(my_y == 0)
-            def _():
-                down_column(lambda to: signal(first_sem, to))
-
-            act(0)
+        peers(act, 1, len(other_rows))
 
     barrier = pltpu.get_barrier_semaphore()
 
@@ -225,12 +221,6 @@
     def entered():
         called = side * cores + side - 2
 
-        @pl.when(is_first)
-        def _():
-            pl.semaphore_wait(barrier, called + side - 1)
-            along_row(lambda to: signal(first_sem, to))
-            down_column(lambda to: signal(first_sem, to))
-
         @pl.when(jnp.logical_not(is_first))
         def _():
             with_first = jnp.logical_or(my_y == 0, below_first)
@@ -247,6 +237,10 @@
 
             down_column(complete)
 
+    for which, table in enumerate((chips, other_rows)):
+        for i, (dx, dy) in enumerate(table):
+            order[2 * which, i] = dx
+            order[2 * which + 1, i] = dy
     small[0].wait()
 
     lane = lax.broadcasted_iota(jnp.int32, (8, 128), 1)
@@ -402,25 +396,75 @@
     lax.fori_loop(0, n * SEA_DEV // 128 // UNROLL, pack, 0)
 
 
-    def exchange(visit, src, dst, rows, k, arrival):
-        def push(to):
-            pltpu.make_async_remote_copy(
-                src_ref=src.at[to, pl.ds(0, rows)],
-                dst_ref=dst.at[me, pl.ds(0, rows)],
-                send_sem=send_sem.at[k],
-                recv_sem=arrival,
-                device_id={"spec": to},
-                device_id_type=MESH,
-            ).start()
-
-        visit(push)
+    def copy_to(to, src, dst, k, arrival):
+        pltpu.make_async_remote_copy(
+            src_ref=src,
+            dst_ref=dst,
+            send_sem=send_sem.at[k],
+            recv_sem=arrival,
+            device_id={"spec": to},
+            device_id_type=MESH,
+        ).start()
+
+    def own_message(src, dst, rows, arrival):
         pltpu.make_async_copy(src.at[me, pl.ds(0, rows)], dst.at[me, pl.ds(0, rows)], arrival).start()
 
     def finish(ref, count, rows, sem):
         part = ref.at[pl.ds(0, count), pl.ds(0, rows)]
         pltpu.make_async_copy(part, part, sem).wait()
 
-    exchange(peers_but_late, send, recv, half, 0, recv_sem.at[my_x])
+    @pl.when(is_first)
+    def _():
+        pl.semaphore_wait(barrier, side * cores + 2 * side - 3)
+        signal(first_sem, 1)
+
+    def push(to):
+        aside = jnp.where(to == 0, 1, 0)
+        copy_to(
+            to + aside,
+            send.at[to, pl.ds(0, half)],
+            recv.at[me + aside * n, pl.ds(0, half)],
+            0,
+            recv_sem.at[my_x + aside * side],
+        )
+
+    def push_own_chip(to):
+        @pl.when(is_second)
+        def _():
+            pltpu.make_async_copy(
+                send.at[0, pl.ds(0, half)], recv.at[n + 1, pl.ds(0, half)], recv_sem.at[side]
+            ).start()
+
+        @pl.when(jnp.logical_not(is_second))
+        def _():
+            copy_to(to, send.at[to, pl.ds(0, half)], recv.at[me, pl.ds(0, half)], 0, recv_sem.at[my_x])
+
+    peers_as_known(push, push_own_chip)
+    own_message(send, recv, half, recv_sem.at[my_x])
+
+    @pl.when(is_second)
+    def _():
+        pl.semaphore_wait(first_sem, 1)
+
+    def hand_over(h):
+        def pass_on(start, count):
+            finish(recv, count, half, recv_sem.at[side + h])
+            copy_to(
+                0,
+                recv.at[pl.ds(n + start, count), pl.ds(0, half)],
+                recv.at[pl.ds(start, count), pl.ds(0, half)],
+                2,
+                recv_sem.at[h],
+            )
+
+        @pl.when(jnp.logical_and(is_second, h != 0))
+        def _():
+            pass_on(h * side * cores, side * cores)
+
+        @pl.when(jnp.logical_and(is_second, h == 0))
+        def _():
+            pass_on(1, side * cores - 1)
+
 
     wind = send[me][half : half + 1, :]
     other = pltpu.roll(wind, SEA_DEV, 1)
@@ -460,6 +504,7 @@
     def arrange(i, carry):
         m0, m1 = carry
         h = lax.rem(i + 1, side)
+        hand_over(h)
         finish(recv, side * cores, half, recv_sem.at[h])
         for g in (2 * h, 2 * h + 1):
             for i in range(group):
@@ -487,8 +532,8 @@
     breaking = steep * steep / (1.0 + steep * steep)
 
     def transfer(g, carry):
-        for q in range(2 * per_group):
-            k = g * 2 * per_group + q
+        for q in range(4 * per_group):
+            k = g * 4 * per_group + q
             a = energy[k]
             factor = tab[pl.ds(at["rate"] + k, 1), :] * a
             rates = []
@@ -500,7 +545,7 @@
             high_part[k] = up[1] + down[1]
         return carry
 
-    lax.fori_loop(0, n // group // 2, transfer, 0)
+    lax.fori_loop(0, n // group // 4, transfer, 0)
 
     def renew(g, total):
         for q in range(per_group):
@@ -526,9 +571,29 @@
 
     lax.fori_loop(0, n // group, add_height, 0)
 
-    exchange(peers, back, home, half + 1, 1, recv_sem.at[side])
-    finish(send, n - 1, half, send_sem.at[0])
-    finish(home, n, half + 1, recv_sem.at[side])
+    def push_back(to):
+        copy_to(
+            to,
+            back.at[to, pl.ds(0, half + 1)],
+            home.at[me, pl.ds(0, half + 1)],
+            1,
+            recv_sem.at[2 * side],
+        )
+
+    peers(push_back, 0, len(chips))
+    own_chip(push_back)
+    own_message(back, home, half + 1, recv_sem.at[2 * side])
+
+    @pl.when(is_second)
+    def _():
+        finish(send, n - 2, half, send_sem.at[0])
+        finish(recv, n - 1, half, send_sem.at[2])
+
+    @pl.when(jnp.logical_not(is_second))
+    def _():
+        finish(send, n - 1, half, send_sem.at[0])
+
+    finish(home, n, half + 1, recv_sem.at[2 * side])
     finish(back, n - 1, half + 1, send_sem.at[1])
 
 
@@ -648,7 +713,7 @@
                 pltpu.VMEM((2, chunks + 2 * FAR, 8, 128), jnp.float32),
                 pltpu.VMEM((2, chunks + 2 * FAR, 8, 128), jnp.float32),
                 messages(n),
-                messages(n),
+                messages(2 * n),
                 messages(n),
                 pltpu.VMEM((n // 8, 8 * bins_dev // 2, 128), jnp.float32),
                 by_freq(NF),
@@ -656,8 +721,9 @@
                 by_freq(NF),
                 by_freq(NF + 2),
                 by_freq(NF + 3),
-                pltpu.SemaphoreType.DMA((2,)),
-                pltpu.SemaphoreType.DMA((side + 1,)),
+                pltpu.SMEM((4, side * side), jnp.int32),
+                pltpu.SemaphoreType.DMA((3,)),
+                pltpu.SemaphoreType.DMA((2 * side + 1,)),
                 pltpu.SemaphoreType.DMA((8,)),
                 pltpu.SemaphoreType.REGULAR((side,)),
                 pltpu.SemaphoreType.REGULAR,

time: 53.6 us -> 52.4 us (0.978)
  Pallas kernels: 52.9 us -> 51.6 us
    pallas_call x1, Pallas kernels: 49.8 us -> 48.6 us  [local(): pl.pallas_call(functools.partial(step_kernel, n, side, cores, at), name='...]
where the time goes in v9:
time: 52.4 us; the launch traced here: 52.3 us
  Pallas kernels  51.6 us (98%)
  between operations  0.65 us (1%)
    pallas_call x1, Pallas kernels, local(): pl.pallas_call(functools.partial(step_kernel, n, side, cores, at), name='...  48.6 us
    pallas_call x1, Pallas kernels, local(): pl.pallas_call(functools.partial(unpack_kernel, n, bins_dev), name='unpac...  3.07 us

profile of v9, /device:TPU:513, one launch (start us, length us, event | category | flops | bytes accessed | tf_op | source)
XLA Modules:
  0.0 52.3 jit_solution(8085841553146441849)
XLA Ops:
  0.6 0.0 copy-start
  0.6 48.6 %wave_step.1 = (f32[128,8,128]{2,1,0:T(8,128)S(1)}, s32[2,160,128]{2,1,0:T(8,128)S(1)}, s32[2,96,128]{2,1,0:T(8,128)S(1)}) custom-call(f32[12,12288]{1,0:T(8,128)} %x_hbm.1, s32[96,128]{1,0:T(8,128)} %bitcast.5, f32[96,128]{1,0:T(8,128)} %bitcast.7, f32[96,128]{1,0:T(8,128)} %bitcast.8, f32[272,128]{1,0:T(8,128)} %constant.2.clone.tab_hbm), custom_call_target="tpu_custom_call" | custom-call | tf_op jit(solution)/shard_map/wave_step/pallas_call | solution.py:690
  49.2 0.0 copy-done
  49.2 3.1 %unpack.1 = (f32[12,12288]{1,0:T(8,128)}, f32[1,96]{1,0:T(1,128)}, f32[1,1]{1,0:T(1,128)}) custom-call(f32[128,8,128]{2,1,0:T(8,128)S(1)} %get-tuple-element.9.home, s32[2,160,128]{2,1,0:T(8,128)S(1)} %get-tuple-element.10.go_right, s32[2,96,128]{2,1,0:T(8,128)S(1)} %get-tuple-element.11.put, s32[96,128]{1,0:T(8,128)S(1)} %bitcast.6), custom_call_target="tpu_custom_call" | custom-call | tf_op jit(solution)/shard_map/unpack/pallas_call | solution.py:747
Async XLA Ops:
  0.6 48.6 %copy-start = (s32[12288]{0:T(1024)S(1)}, s32[12288]{0:T(1024)}, u32[]{:S(2)}) copy-start(s32[12288]{0:T(1024)} %param.6) | copy-start | bytes 147460

commit v10 on v9

--- a/solution.py
+++ b/solution.py
@@ -93,16 +93,20 @@
     lax.fori_loop(0, chunks // UNROLL, block, 0)
 
 
-def far_rows(words, src, t, v, way, bit_order):
-    def value(v, order):
-        if not order:
-            return src[t, FAR + v]
-        d = way * (1 << order[-1])
-        return jnp.where(
-            has(word_of(words.at[t], v), order[-1]), value(v + d, order[:-1]), value(v, order[:-1])
-        )
-
-    return value(v, bit_order)
+def far_rows(chunks, words, tiles, t, r, toward_end, bit_order):
+    tiles = tiles + [None] * (chunks // 8 - len(tiles))
+    word = [word_of(words.at[t], r + 8 * j) for j in range(chunks // 8)]
+    for b in bit_order:
+        d = (1 << (b - 3)) * (1 if toward_end else -1)
+        moved = []
+        for j, own in enumerate(tiles):
+            other = tiles[j + d] if 0 <= j + d < len(tiles) else None
+            if own is None or other is None:
+                moved.append(other if own is None else own)
+            else:
+                moved.append(jnp.where(has(word[j], b), other, own))
+        tiles = moved
+    return tiles
 
 
 def step_kernel(
@@ -305,16 +309,23 @@
     base = (me * bins_dev) % ND
     for copy in small[1:]:
         copy.wait()
-    cw, ce, cs, cn = [], [], [], []
+    pace_x, pace_y, from_west, from_south, beside, edge = [], [], [], [], [], []
     for t in range(2):
         k = ((me * bins_dev + jnp.minimum(2 * row + t, bins_dev - 1)) // ND).astype(jnp.float32)
         pace = 0.2 * jnp.exp(-LOG_RATIO * k)
         ax = pace * tab[pl.ds(at["cos"] + base + t, 8, stride=2), :]
         ay = pace * tab[pl.ds(at["sin"] + base + t, 8, stride=2), :]
-        cw.append(jnp.maximum(ax, 0.0))
-        ce.append(-jnp.minimum(ax, 0.0))
-        cs.append(jnp.maximum(ay, 0.0))
-        cn.append(-jnp.minimum(ay, 0.0))
+        pace_x.append(jnp.abs(ax))
+        pace_y.append(jnp.abs(ay))
+        from_west.append(ax >= 0.0)
+        from_south.append(ay >= 0.0)
+        beside.append(jnp.bitwise_and(jnp.where(from_west[t], lane - 1, lane + 1), 127))
+        edge.append(
+            (
+                jnp.logical_and(from_west[t], lane == 0),
+                jnp.logical_and(jnp.logical_not(from_west[t]), lane == 127),
+            )
+        )
 
     def split_bins(g, carry):
         for u in range(8):
@@ -343,19 +354,18 @@
                 widen = tab[pl.ds(at["widen"] + r, 1), :]
                 first = pad + r * per_row
                 for t in range(2):
-                    west_c, east_c = cw[t] * widen, ce[t] * widen
-                    own_c = 1.0 - west_c - east_c - cs[t] - cn[t]
+                    side_c = pace_x[t] * widen
+                    own_c = 1.0 - side_c - pace_y[t]
+                    first = pad + r * per_row
                     e = [src[t, first + q] for q in range(per_row)]
-                    right = [pltpu.roll(a, 1, 1) for a in e]
-                    left = [pltpu.roll(a, 127, 1) for a in e]
+                    turned = [jnp.take_along_axis(a, beside[t], axis=1, mode="promise_in_bounds") for a in e]
                     for q in range(per_row):
-                        west = jnp.where(lane == 0, right[q - 1], right[q])
-                        east = jnp.where(lane == 127, left[(q + 1) % per_row], left[q])
-                        new = (
-                            own_c * e[q] + west_c * west + east_c * east
-                            + cs[t] * src[t, first + q - per_row]
-                            + cn[t] * src[t, first + q + per_row]
+                        across = jnp.where(edge[t][0], turned[q - 1], turned[q])
+                        across = jnp.where(edge[t][1], turned[(q + 1) % per_row], across)
+                        along = jnp.where(
+                            from_south[t], src[t, first + q - per_row], src[t, first + q + per_row]
                         )
+                        new = own_c * e[q] + side_c * across + pace_y[t] * along
                         v = first + q - pad
                         if s < SUBSTEPS - 1:
                             dst[t, first + q] = new * sea_float[pl.ds(v, 1), :]
@@ -385,16 +395,24 @@
 
     near_rows(chunks, go_left, moved_a, keep_near, True, (0, 1, 2))
 
-    def pack(g, carry):
-        for u in range(UNROLL):
-            v = g * UNROLL + u
-            even, odd = (far_rows(go_left, moved_b, t, v, 1, (3, 4, 5)) for t in range(2))
-            send[2 * v] = jnp.where(low, even, odd)
-            send[2 * v + 1] = jnp.where(low, odd, even)
+    def pack(r, carry):
+        even, odd = (
+            far_rows(
+                chunks, go_left, [moved_b[t, FAR + r + 8 * j] for j in range(chunks // 8)], t, r, True, (3, 4, 5)
+            )
+            for t in range(2)
+        )
+        for j in range(n * SEA_DEV // 128 // 8):
+            v = r + 8 * j
+            send[2 * v] = jnp.where(low, even[j], odd[j])
+            send[2 * v + 1] = jnp.where(low, odd[j], even[j])
         return carry
 
-    lax.fori_loop(0, n * SEA_DEV // 128 // UNROLL, pack, 0)
-
+    lax.fori_loop(0, 8, pack, 0)
+
+    def finish(ref, count, rows, sem):
+        part = ref.at[pl.ds(0, count), pl.ds(0, rows)]
+        pltpu.make_async_copy(part, part, sem).wait()
 
     def copy_to(to, src, dst, k, arrival):
         pltpu.make_async_remote_copy(
@@ -408,10 +426,6 @@
 
     def own_message(src, dst, rows, arrival):
         pltpu.make_async_copy(src.at[me, pl.ds(0, rows)], dst.at[me, pl.ds(0, rows)], arrival).start()
-
-    def finish(ref, count, rows, sem):
-        part = ref.at[pl.ds(0, count), pl.ds(0, rows)]
-        pltpu.make_async_copy(part, part, sem).wait()
 
     @pl.when(is_first)
     def _():
@@ -601,7 +615,7 @@
     n, bins_dev,
     home, go_right, put, mask2d,
     out, height_out, mean_out,
-    moved_a, moved_b, stage, heights,
+    moved_a, moved_b, stage, heights, result, own_heights, mean, write_sem,
 ):
     chunks = mask2d.shape[0]
     half = bins_dev // 2
@@ -611,29 +625,26 @@
     lane = lax.broadcasted_iota(jnp.int32, (8, 128), 1)
     low = lane < SEA_DEV
 
-    def unpack(g, carry):
-        for u in range(2 * UNROLL):
-            v = g * 2 * UNROLL + u
-            a, b = home[2 * v], home[2 * v + 1]
-            moved_a[0, FAR + v] = jnp.where(low, a, b)
-            moved_a[1, FAR + v] = jnp.where(low, b, a)
+    def spread(r, carry):
+        pairs = [(home[2 * (r + 8 * j)], home[2 * (r + 8 * j) + 1]) for j in range(n * SEA_DEV // 128 // 8)]
+        for t in range(2):
+            tiles = [jnp.where(low, p[t], p[1 - t]) for p in pairs]
+            for j, tile in enumerate(far_rows(chunks, go_right, tiles, t, r, False, (5, 4, 3))):
+                moved_b[t, FAR + r + 8 * j] = tile
         return carry
 
-    lax.fori_loop(0, n * SEA_DEV // 128 // (2 * UNROLL), unpack, 0)
-
-    def spread(g, carry):
-        for u in range(4):
-            v = g * 4 + u
-            for t in range(2):
-                moved_b[t, FAR + v] = far_rows(go_right, moved_a, t, v, -1, (5, 4, 3))
-        return carry
-
-    lax.fori_loop(0, chunks // 4, spread, 0)
+    lax.fori_loop(0, 8, spread, 0)
 
     def keep_apart(t, u, v, tile):
         moved_a[t, FAR + v] = tile
 
     near_rows(chunks, go_right, moved_b, keep_apart, False, (2, 1, 0))
+
+    width = 2 * UNROLL * 128
+
+    def write(g):
+        cols = pl.ds(pl.multiple_of(g * width, 128), width)
+        return pltpu.make_async_copy(result.at[:, cols], out.at[:, cols], write_sem.at[g])
 
     def deliver(g, carry):
         for u in range(2 * UNROLL):
@@ -646,7 +657,8 @@
                     heights[pl.ds(v, 1), :] = tile[half : half + 1]
         for u in range(2 * UNROLL):
             v = g * 2 * UNROLL + u
-            out[:, pl.ds(pl.multiple_of(v * 128, 128), 128)] = stage[u, 0:bins_dev, :]
+            result[:, pl.ds(pl.multiple_of(v * 128, 128), 128)] = stage[u, 0:bins_dev, :]
+        write(g).start()
         return carry
 
     lax.fori_loop(0, chunks // (2 * UNROLL), deliver, 0)
@@ -668,9 +680,24 @@
                 pltpu.roll(after, 128 - offset, 1),
             )
         picked = piece if picked is None else jnp.where(u == g, piece, picked)
-    height_out[...] = picked[:, 0:points]
+    own_heights[...] = picked[:, 0:points]
     all_heights = jnp.sum(heights[...], axis=0, keepdims=True)
-    mean_out[...] = jnp.sum(all_heights, axis=1, keepdims=True) * (1.0 / (SEA_DEV * n))
+    mean[...] = jnp.sum(all_heights, axis=1, keepdims=True) * (1.0 / (SEA_DEV * n))
+
+    small = (
+        pltpu.make_async_copy(own_heights, height_out, write_sem.at[cells // width]),
+        pltpu.make_async_copy(mean, mean_out, write_sem.at[cells // width + 1]),
+    )
+    for copy in small:
+        copy.start()
+
+    def written(g, carry):
+        write(g).wait()
+        return carry
+
+    lax.fori_loop(0, cells // width, written, 0)
+    for copy in small:
+        copy.wait()
 
 
 def solution(mesh):
@@ -753,12 +780,16 @@
                 jax.ShapeDtypeStruct((1, 1), jnp.float32),
             ),
             in_specs=[vmem] * 4,
-            out_specs=(vmem,) * 3,
+            out_specs=(pl.BlockSpec(memory_space=pl.ANY),) * 3,
             scratch_shapes=[
                 moved,
                 moved,
                 pltpu.VMEM((16, 16, 128), jnp.float32),
                 pltpu.VMEM((chunks, 128), jnp.float32),
+                pltpu.VMEM((bins_dev, cells), jnp.float32),
+                pltpu.VMEM((1, cells // n), jnp.float32),
+                pltpu.VMEM((1, 1), jnp.float32),
+                pltpu.SemaphoreType.DMA((chunks // (2 * UNROLL) + 2,)),
             ],
             compiler_params=pltpu.CompilerParams(vmem_limit_bytes=VMEM_BYTES),
         )(home, go_right, put, sea_mask.reshape(chunks, 128))

time: 52.4 us -> 51.4 us (0.981)
  Pallas kernels: 51.6 us -> 50.6 us
    pallas_call x1, Pallas kernels: 3.07 us -> 2.33 us  [local(): pl.pallas_call(functools.partial(unpack_kernel, n, bins_dev), name='unpac...]
where the time goes in v10:
time: 51.4 us; the launch traced here: 51.2 us
  Pallas kernels  50.6 us (98%)
  between operations  0.65 us (1%)
    pallas_call x1, Pallas kernels, local(): pl.pallas_call(functools.partial(step_kernel, n, side, cores, at), name='...  48.2 us
    pallas_call x1, Pallas kernels, local(): pl.pallas_call(functools.partial(unpack_kernel, n, bins_dev), name='unpac...  2.33 us

profile of v10, /device:TPU:513, one launch (start us, length us, event | category | flops | bytes accessed | tf_op | source)
XLA Modules:
  0.0 51.2 jit_solution(4547876830751284442)
XLA Ops:
  0.6 0.0 copy-start
  0.6 48.2 %wave_step.1 = (f32[128,8,128]{2,1,0:T(8,128)S(1)}, s32[2,160,128]{2,1,0:T(8,128)S(1)}, s32[2,96,128]{2,1,0:T(8,128)S(1)}) custom-call(f32[12,12288]{1,0:T(8,128)} %x_hbm.1, s32[96,128]{1,0:T(8,128)} %bitcast.5, f32[96,128]{1,0:T(8,128)} %bitcast.7, f32[96,128]{1,0:T(8,128)} %bitcast.8, f32[272,128]{1,0:T(8,128)} %constant.2.clone.tab_hbm), custom_call_target="tpu_custom_call" | custom-call | tf_op jit(solution)/shard_map/wave_step/pallas_call | solution.py:717
  48.9 0.0 copy-done
  48.9 2.3 %unpack.1 = (f32[12,12288]{1,0:T(8,128)}, f32[1,96]{1,0:T(1,128)}, f32[1,1]{1,0:T(1,128)}) custom-call(f32[128,8,128]{2,1,0:T(8,128)S(1)} %get-tuple-element.9.home, s32[2,160,128]{2,1,0:T(8,128)S(1)} %get-tuple-element.10.go_right, s32[2,96,128]{2,1,0:T(8,128)S(1)} %get-tuple-element.11.put, s32[96,128]{1,0:T(8,128)S(1)} %bitcast.6), custom_call_target="tpu_custom_call" | custom-call | tf_op jit(solution)/shard_map/unpack/pallas_call | solution.py:774
Async XLA Ops:
  0.6 48.3 %copy-start = (s32[12288]{0:T(1024)S(1)}, s32[12288]{0:T(1024)}, u32[]{:S(2)}) copy-start(s32[12288]{0:T(1024)} %param.6) | copy-start | bytes 147460

commit v11 on v10

--- a/solution.py
+++ b/solution.py
@@ -381,13 +381,13 @@
     entered()
 
     def to_lanes(g, carry):
-        for u in range(2 * UNROLL):
-            v = g * 2 * UNROLL + u
+        for u in range(4 * UNROLL):
+            v = g * 4 * UNROLL + u
             for t in range(2):
                 moved_a[t, FAR + v] = lanes(final[t, pad + v], pick.at[t], v)
         return carry
 
-    lax.fori_loop(0, chunks // (2 * UNROLL), to_lanes, 0)
+    lax.fori_loop(0, chunks // (4 * UNROLL), to_lanes, 0)
 
 
     def keep_near(t, u, v, tile):
@@ -647,21 +647,22 @@
         return pltpu.make_async_copy(result.at[:, cols], out.at[:, cols], write_sem.at[g])
 
     def deliver(g, carry):
-        for u in range(2 * UNROLL):
-            v = g * 2 * UNROLL + u
+        for u in range(4 * UNROLL):
+            v = g * 4 * UNROLL + u
             sea = jnp.broadcast_to(mask2d[pl.ds(v, 1), :] != 0, (8, 128))
             for t in range(2):
                 tile = jnp.where(sea, lanes(moved_a[t, FAR + v], put.at[t], v), 0.0)
                 stage[u, pl.ds(t, half, stride=2), :] = tile[0:half]
                 if t == 0:
                     heights[pl.ds(v, 1), :] = tile[half : half + 1]
-        for u in range(2 * UNROLL):
-            v = g * 2 * UNROLL + u
-            result[:, pl.ds(pl.multiple_of(v * 128, 128), 128)] = stage[u, 0:bins_dev, :]
-        write(g).start()
+        for part in range(2):
+            for u in range(part * 2 * UNROLL, (part + 1) * 2 * UNROLL):
+                v = g * 4 * UNROLL + u
+                result[:, pl.ds(pl.multiple_of(v * 128, 128), 128)] = stage[u, 0:bins_dev, :]
+            write(2 * g + part).start()
         return carry
 
-    lax.fori_loop(0, chunks // (2 * UNROLL), deliver, 0)
+    lax.fori_loop(0, chunks // (4 * UNROLL), deliver, 0)
 
     points = cells // n
     together = NLON // points
@@ -784,7 +785,7 @@
             scratch_shapes=[
                 moved,
                 moved,
-                pltpu.VMEM((16, 16, 128), jnp.float32),
+                pltpu.VMEM((32, 16, 128), jnp.float32),
                 pltpu.VMEM((chunks, 128), jnp.float32),
                 pltpu.VMEM((bins_dev, cells), jnp.float32),
                 pltpu.VMEM((1, cells // n), jnp.float32),

time: 51.4 us -> 51 us (level)
  no operation moved by 1% of the time
where the time goes in v11:
time: 51 us; the launch traced here: 50.8 us
  Pallas kernels  50.2 us (98%)
  between operations  0.65 us (1%)
    pallas_call x1, Pallas kernels, local(): pl.pallas_call(functools.partial(step_kernel, n, side, cores, at), name='...  48 us
    pallas_call x1, Pallas kernels, local(): pl.pallas_call(functools.partial(unpack_kernel, n, bins_dev), name='unpac...  2.13 us

profile of v11, /device:TPU:513, one launch (start us, length us, event | category | flops | bytes accessed | tf_op | source)
XLA Modules:
  0.0 50.8 jit_solution(1197306701723177176)
XLA Ops:
  0.6 0.0 copy-start
  0.6 48.0 %wave_step.1 = (f32[128,8,128]{2,1,0:T(8,128)S(1)}, s32[2,160,128]{2,1,0:T(8,128)S(1)}, s32[2,96,128]{2,1,0:T(8,128)S(1)}) custom-call(f32[12,12288]{1,0:T(8,128)} %x_hbm.1, s32[96,128]{1,0:T(8,128)} %bitcast.5, f32[96,128]{1,0:T(8,128)} %bitcast.7, f32[96,128]{1,0:T(8,128)} %bitcast.8, f32[272,128]{1,0:T(8,128)} %constant.2.clone.tab_hbm), custom_call_target="tpu_custom_call" | custom-call | tf_op jit(solution)/shard_map/wave_step/pallas_call | solution.py:718
  48.7 0.0 copy-done
  48.7 2.1 %unpack.1 = (f32[12,12288]{1,0:T(8,128)}, f32[1,96]{1,0:T(1,128)}, f32[1,1]{1,0:T(1,128)}) custom-call(f32[128,8,128]{2,1,0:T(8,128)S(1)} %get-tuple-element.9.home, s32[2,160,128]{2,1,0:T(8,128)S(1)} %get-tuple-element.10.go_right, s32[2,96,128]{2,1,0:T(8,128)S(1)} %get-tuple-element.11.put, s32[96,128]{1,0:T(8,128)S(1)} %bitcast.6), custom_call_target="tpu_custom_call" | custom-call | tf_op jit(solution)/shard_map/unpack/pallas_call | solution.py:775
Async XLA Ops:
  0.6 48.1 %copy-start = (s32[12288]{0:T(1024)S(1)}, s32[12288]{0:T(1024)}, u32[]{:S(2)}) copy-start(s32[12288]{0:T(1024)} %param.6) | copy-start | bytes 147460

commit v12 on v11

--- a/solution.py
+++ b/solution.py
@@ -114,7 +114,7 @@
     x_hbm, mask_hbm, speed_hbm, angle_hbm, tab_hbm,
     home, go_right, put,
     x, mask2d, sea_float, speed2d, angle2d, tab, field_a, field_b, stage, shifts, go_left, pick, moved_a, moved_b,
-    send, recv, back, flat, energy, rolled, own, low_part, high_part,
+    send, recv, back, swap, flat, energy, rolled, own, low_part, high_part,
     order, send_sem, recv_sem, load_sem, column_sem, first_sem,
 ):
     bins_dev, cells = x.shape
@@ -578,25 +578,42 @@
     total = lax.fori_loop(0, n // group, renew, zero16)
     height = 4.0 * jnp.sqrt(over_bins(total) + 1e-6)
 
+    swap[0, 0:1, :] = height
+    partner = me + 1 - 2 * my_c
+    copy_to(partner, swap.at[0, pl.ds(0, 1)], swap.at[1, pl.ds(0, 1)], 4, recv_sem.at[2 * side + 2])
+
+    def push_back(to, rows, k):
+        copy_to(
+            to,
+            back.at[to, pl.ds(0, rows)],
+            home.at[me, pl.ds(0, rows)],
+            (1, 3)[k],
+            recv_sem.at[2 * side + k],
+        )
+
+    def on_core(core, rows, k):
+        def chip(i, carry):
+            px, py = wrap(my_x + order[0, i]), wrap(my_y + order[1, i])
+            push_back((px * side + py) * cores + core, rows, k)
+            return carry
+
+        lax.fori_loop(0, len(chips), chip, 0)
+
+    on_core(1 - my_c, half, 0)
+    push_back(partner, half, 0)
+    swapped = swap.at[1, pl.ds(0, 1)]
+    pltpu.make_async_copy(swapped, swapped, recv_sem.at[2 * side + 2]).wait()
+    theirs = swap[1, 0:1, :]
+    both_heights = jnp.where(even_half((1, 128)), height, theirs)
+
     def add_height(g, carry):
         for i in range(group):
-            back[g * group + i, half : half + 1, :] = height
+            back[g * group + i, half : half + 1, :] = both_heights
         return carry
 
     lax.fori_loop(0, n // group, add_height, 0)
-
-    def push_back(to):
-        copy_to(
-            to,
-            back.at[to, pl.ds(0, half + 1)],
-            home.at[me, pl.ds(0, half + 1)],
-            1,
-            recv_sem.at[2 * side],
-        )
-
-    peers(push_back, 0, len(chips))
-    own_chip(push_back)
-    own_message(back, home, half + 1, recv_sem.at[2 * side])
+    on_core(my_c, half + 1, 1)
+    own_message(back, home, half + 1, recv_sem.at[2 * side + 1])
 
     @pl.when(is_second)
     def _():
@@ -607,8 +624,11 @@
     def _():
         finish(send, n - 1, half, send_sem.at[0])
 
-    finish(home, n, half + 1, recv_sem.at[2 * side])
-    finish(back, n - 1, half + 1, send_sem.at[1])
+    finish(home, n // cores, half, recv_sem.at[2 * side])
+    finish(home, n // cores, half + 1, recv_sem.at[2 * side + 1])
+    finish(back, n // cores, half, send_sem.at[1])
+    finish(back, n // cores - 1, half + 1, send_sem.at[3])
+    pltpu.make_async_copy(swapped, swapped, send_sem.at[4]).wait()
 
 
 def unpack_kernel(
@@ -625,10 +645,14 @@
     lane = lax.broadcasted_iota(jnp.int32, (8, 128), 1)
     low = lane < SEA_DEV
 
+    row = lax.broadcasted_iota(jnp.int32, (8, 128), 0)
+    own_core = jnp.where(lax.rem(me, 2) == 0, 0, SEA_DEV)
+    from_even = (jnp.where(row == half, own_core, lane) < SEA_DEV, jnp.logical_not(low))
+
     def spread(r, carry):
         pairs = [(home[2 * (r + 8 * j)], home[2 * (r + 8 * j) + 1]) for j in range(n * SEA_DEV // 128 // 8)]
         for t in range(2):
-            tiles = [jnp.where(low, p[t], p[1 - t]) for p in pairs]
+            tiles = [jnp.where(from_even[t], p[0], p[1]) for p in pairs]
             for j, tile in enumerate(far_rows(chunks, go_right, tiles, t, r, False, (5, 4, 3))):
                 moved_b[t, FAR + r + 8 * j] = tile
         return carry
@@ -743,6 +767,7 @@
                 messages(n),
                 messages(2 * n),
                 messages(n),
+                messages(2),
                 pltpu.VMEM((n // 8, 8 * bins_dev // 2, 128), jnp.float32),
                 by_freq(NF),
                 by_freq(4, NF + 5),
@@ -750,8 +775,8 @@
                 by_freq(NF + 2),
                 by_freq(NF + 3),
                 pltpu.SMEM((4, side * side), jnp.int32),
-                pltpu.SemaphoreType.DMA((3,)),
-                pltpu.SemaphoreType.DMA((2 * side + 1,)),
+                pltpu.SemaphoreType.DMA((5,)),
+                pltpu.SemaphoreType.DMA((2 * side + 3,)),
                 pltpu.SemaphoreType.DMA((8,)),
                 pltpu.SemaphoreType.REGULAR((side,)),
                 pltpu.SemaphoreType.REGULAR,

time: 51 us -> 49.9 us (0.978)
  Pallas kernels: 50.2 us -> 49.2 us
    pallas_call x1, Pallas kernels: 48 us -> 47 us  [local(): pl.pallas_call(functools.partial(step_kernel, n, side, cores, at), name='...]
where the time goes in v12:
time: 49.9 us; the launch traced here: 49.8 us
  Pallas kernels  49.2 us (99%)
  between operations  0.65 us (1%)
    pallas_call x1, Pallas kernels, local(): pl.pallas_call(functools.partial(step_kernel, n, side, cores, at), name='...  47 us
    pallas_call x1, Pallas kernels, local(): pl.pallas_call(functools.partial(unpack_kernel, n, bins_dev), name='unpac...  2.13 us

profile of v12, /device:TPU:513, one launch (start us, length us, event | category | flops | bytes accessed | tf_op | source)
XLA Modules:
  0.0 49.8 jit_solution(9628354467143204117)
XLA Ops:
  0.6 0.0 copy-start
  0.6 47.0 %wave_step.1 = (f32[128,8,128]{2,1,0:T(8,128)S(1)}, s32[2,160,128]{2,1,0:T(8,128)S(1)}, s32[2,96,128]{2,1,0:T(8,128)S(1)}) custom-call(f32[12,12288]{1,0:T(8,128)} %x_hbm.1, s32[96,128]{1,0:T(8,128)} %bitcast.5, f32[96,128]{1,0:T(8,128)} %bitcast.7, f32[96,128]{1,0:T(8,128)} %bitcast.8, f32[272,128]{1,0:T(8,128)} %constant.2.clone.tab_hbm), custom_call_target="tpu_custom_call" | custom-call | tf_op jit(solution)/shard_map/wave_step/pallas_call | solution.py:742
  47.7 0.0 copy-done
  47.7 2.1 %unpack.1 = (f32[12,12288]{1,0:T(8,128)}, f32[1,96]{1,0:T(1,128)}, f32[1,1]{1,0:T(1,128)}) custom-call(f32[128,8,128]{2,1,0:T(8,128)S(1)} %get-tuple-element.9.home, s32[2,160,128]{2,1,0:T(8,128)S(1)} %get-tuple-element.10.go_right, s32[2,96,128]{2,1,0:T(8,128)S(1)} %get-tuple-element.11.put, s32[96,128]{1,0:T(8,128)S(1)} %bitcast.6), custom_call_target="tpu_custom_call" | custom-call | tf_op jit(solution)/shard_map/unpack/pallas_call | solution.py:800
Async XLA Ops:
  0.6 47.0 %copy-start = (s32[12288]{0:T(1024)S(1)}, s32[12288]{0:T(1024)}, u32[]{:S(2)}) copy-start(s32[12288]{0:T(1024)} %param.6) | copy-start | bytes 147460

commit v13 on v12

--- a/solution.py
+++ b/solution.py
@@ -348,9 +348,10 @@
 
         def advance(g, to_go, src=src, dst=dst, s=s):
             if s == 0:
-                to_go = close_up(2 * g + 1, close_up(2 * g, to_go))
-            for ru in range(8):
-                r = g * 8 + ru
+                for i in range(4):
+                    to_go = close_up(4 * g + i, to_go)
+            for ru in range(16):
+                r = g * 16 + ru
                 widen = tab[pl.ds(at["widen"] + r, 1), :]
                 first = pad + r * per_row
                 for t in range(2):
@@ -374,7 +375,7 @@
                             dst[t, first + q] = jnp.where(row == half, wind, new)
             return to_go
 
-        to_go = lax.fori_loop(0, lat_count // 8, advance, to_go)
+        to_go = lax.fori_loop(0, lat_count // 16, advance, to_go)
         if s == 0:
             plan_rows(to_go)
     final = field_a if SUBSTEPS % 2 == 0 else field_b
@@ -561,21 +562,23 @@
 
     lax.fori_loop(0, n // group // 4, transfer, 0)
 
-    def renew(g, total):
-        for q in range(per_group):
-            k = g * per_group + q
-            a = energy[k]
-            omega = tab[pl.ds(at["omega"] + k, 1), :]
-            gain = (0.05 * omega) * jnp.maximum(0.0, omega * toward - 1.0)
-            new = a + (gain - (0.03 * omega) * breaking) * a
-            new = new + own[k] + low_part[k] + high_part[k + 3]
-            total = total + new
-            flat[g, PAIRS * q : PAIRS * (q + 1), :] = new
-        for i in range(group):
-            back[g * group + i, 0:half, :] = flat[g, half * i : half * i + half, :]
+    def renew(h, total):
+        for g in (2 * h, 2 * h + 1):
+            for q in range(per_group):
+                k = g * per_group + q
+                a = energy[k]
+                omega = tab[pl.ds(at["omega"] + k, 1), :]
+                gain = (0.05 * omega) * jnp.maximum(0.0, omega * toward - 1.0)
+                new = a + (gain - (0.03 * omega) * breaking) * a
+                new = new + own[k] + low_part[k] + high_part[k + 3]
+                total = total + new
+                flat[g, PAIRS * q : PAIRS * (q + 1), :] = new
+        for g in (2 * h, 2 * h + 1):
+            for i in range(group):
+                back[g * group + i, 0:half, :] = flat[g, half * i : half * i + half, :]
         return total
 
-    total = lax.fori_loop(0, n // group, renew, zero16)
+    total = lax.fori_loop(0, n // group // 2, renew, zero16)
     height = 4.0 * jnp.sqrt(over_bins(total) + 1e-6)
 
     swap[0, 0:1, :] = height

time: 49.9 us -> 49.7 us (level)
  no operation moved by 1% of the time
where the time goes in v13:
time: 49.7 us; the launch traced here: 49.6 us
  Pallas kernels  48.9 us (98%)
  between operations  0.65 us (1%)
    pallas_call x1, Pallas kernels, local(): pl.pallas_call(functools.partial(step_kernel, n, side, cores, at), name='...  46.8 us
    pallas_call x1, Pallas kernels, local(): pl.pallas_call(functools.partial(unpack_kernel, n, bins_dev), name='unpac...  2.13 us

profile of v13, /device:TPU:513, one launch (start us, length us, event | category | flops | bytes accessed | tf_op | source)
XLA Modules:
  0.0 49.6 jit_solution(12548755984060377406)
XLA Ops:
  0.6 0.0 copy-start
  0.6 46.8 %wave_step.1 = (f32[128,8,128]{2,1,0:T(8,128)S(1)}, s32[2,160,128]{2,1,0:T(8,128)S(1)}, s32[2,96,128]{2,1,0:T(8,128)S(1)}) custom-call(f32[12,12288]{1,0:T(8,128)} %x_hbm.1, s32[96,128]{1,0:T(8,128)} %bitcast.5, f32[96,128]{1,0:T(8,128)} %bitcast.7, f32[96,128]{1,0:T(8,128)} %bitcast.8, f32[272,128]{1,0:T(8,128)} %constant.2.clone.tab_hbm), custom_call_target="tpu_custom_call" | custom-call | tf_op jit(solution)/shard_map/wave_step/pallas_call | solution.py:745
  47.5 0.0 copy-done
  47.5 2.1 %unpack.1 = (f32[12,12288]{1,0:T(8,128)}, f32[1,96]{1,0:T(1,128)}, f32[1,1]{1,0:T(1,128)}) custom-call(f32[128,8,128]{2,1,0:T(8,128)S(1)} %get-tuple-element.9.home, s32[2,160,128]{2,1,0:T(8,128)S(1)} %get-tuple-element.10.go_right, s32[2,96,128]{2,1,0:T(8,128)S(1)} %get-tuple-element.11.put, s32[96,128]{1,0:T(8,128)S(1)} %bitcast.6), custom_call_target="tpu_custom_call" | custom-call | tf_op jit(solution)/shard_map/unpack/pallas_call | solution.py:803
Async XLA Ops:
  0.6 46.8 %copy-start = (s32[12288]{0:T(1024)S(1)}, s32[12288]{0:T(1024)}, u32[]{:S(2)}) copy-start(s32[12288]{0:T(1024)} %param.6) | copy-start | bytes 147460

commit v14 on v13

--- a/solution.py
+++ b/solution.py
@@ -382,13 +382,13 @@
     entered()
 
     def to_lanes(g, carry):
-        for u in range(4 * UNROLL):
-            v = g * 4 * UNROLL + u
+        for u in range(6 * UNROLL):
+            v = g * 6 * UNROLL + u
             for t in range(2):
                 moved_a[t, FAR + v] = lanes(final[t, pad + v], pick.at[t], v)
         return carry
 
-    lax.fori_loop(0, chunks // (4 * UNROLL), to_lanes, 0)
+    lax.fori_loop(0, chunks // (6 * UNROLL), to_lanes, 0)
 
 
     def keep_near(t, u, v, tile):
@@ -674,22 +674,22 @@
         return pltpu.make_async_copy(result.at[:, cols], out.at[:, cols], write_sem.at[g])
 
     def deliver(g, carry):
-        for u in range(4 * UNROLL):
-            v = g * 4 * UNROLL + u
+        for u in range(6 * UNROLL):
+            v = g * 6 * UNROLL + u
             sea = jnp.broadcast_to(mask2d[pl.ds(v, 1), :] != 0, (8, 128))
             for t in range(2):
                 tile = jnp.where(sea, lanes(moved_a[t, FAR + v], put.at[t], v), 0.0)
                 stage[u, pl.ds(t, half, stride=2), :] = tile[0:half]
                 if t == 0:
                     heights[pl.ds(v, 1), :] = tile[half : half + 1]
-        for part in range(2):
+        for part in range(3):
             for u in range(part * 2 * UNROLL, (part + 1) * 2 * UNROLL):
-                v = g * 4 * UNROLL + u
+                v = g * 6 * UNROLL + u
                 result[:, pl.ds(pl.multiple_of(v * 128, 128), 128)] = stage[u, 0:bins_dev, :]
-            write(2 * g + part).start()
+            write(3 * g + part).start()
         return carry
 
-    lax.fori_loop(0, chunks // (4 * UNROLL), deliver, 0)
+    lax.fori_loop(0, chunks // (6 * UNROLL), deliver, 0)
 
     points = cells // n
     together = NLON // points
@@ -813,7 +813,7 @@
             scratch_shapes=[
                 moved,
                 moved,
-                pltpu.VMEM((32, 16, 128), jnp.float32),
+                pltpu.VMEM((48, 16, 128), jnp.float32),
                 pltpu.VMEM((chunks, 128), jnp.float32),
                 pltpu.VMEM((bins_dev, cells), jnp.float32),
                 pltpu.VMEM((1, cells // n), jnp.float32),

time: 49.7 us -> 49.6 us (level)
  no operation moved by 1% of the time
where the time goes in v14:
time: 49.6 us; the launch traced here: 49.4 us
  Pallas kernels  48.8 us (98%)
  between operations  0.65 us (1%)
    pallas_call x1, Pallas kernels, local(): pl.pallas_call(functools.partial(step_kernel, n, side, cores, at), name='...  46.7 us
    pallas_call x1, Pallas kernels, local(): pl.pallas_call(functools.partial(unpack_kernel, n, bins_dev), name='unpac...  2.07 us

profile of v14, /device:TPU:513, one launch (start us, length us, event | category | flops | bytes accessed | tf_op | source)
XLA Modules:
  0.0 49.4 jit_solution(2491575835013553925)
XLA Ops:
  0.6 0.0 copy-start
  0.6 46.7 %wave_step.1 = (f32[128,8,128]{2,1,0:T(8,128)S(1)}, s32[2,160,128]{2,1,0:T(8,128)S(1)}, s32[2,96,128]{2,1,0:T(8,128)S(1)}) custom-call(f32[12,12288]{1,0:T(8,128)} %x_hbm.1, s32[96,128]{1,0:T(8,128)} %bitcast.5, f32[96,128]{1,0:T(8,128)} %bitcast.7, f32[96,128]{1,0:T(8,128)} %bitcast.8, f32[272,128]{1,0:T(8,128)} %constant.2.clone.tab_hbm), custom_call_target="tpu_custom_call" | custom-call | tf_op jit(solution)/shard_map/wave_step/pallas_call | solution.py:745
  47.4 0.0 copy-done
  47.4 2.1 %unpack.1 = (f32[12,12288]{1,0:T(8,128)}, f32[1,96]{1,0:T(1,128)}, f32[1,1]{1,0:T(1,128)}) custom-call(f32[128,8,128]{2,1,0:T(8,128)S(1)} %get-tuple-element.9.home, s32[2,160,128]{2,1,0:T(8,128)S(1)} %get-tuple-element.10.go_right, s32[2,96,128]{2,1,0:T(8,128)S(1)} %get-tuple-element.11.put, s32[96,128]{1,0:T(8,128)S(1)} %bitcast.6), custom_call_target="tpu_custom_call" | custom-call | tf_op jit(solution)/shard_map/unpack/pallas_call | solution.py:803
Async XLA Ops:
  0.6 46.7 %copy-start = (s32[12288]{0:T(1024)S(1)}, s32[12288]{0:T(1024)}, u32[]{:S(2)}) copy-start(s32[12288]{0:T(1024)} %param.6) | copy-start | bytes 147460
